TPU v7x, 32 devices: a 4x4x1 block of a 4x4x8 slice. The times are simulated.
32 devices in a mesh: dp: 1 (over z), sp2: 4 (over y), sp: 8 (over x, core).
Axes of the slice: x: 4, y: 4, z: 1, core: 2. Of those that a mesh axis runs over, the one named last changes fastest.
The devices are a block of a 4x4x8 slice.
Arguments:
- x: bfloat16 [8, 64, 512, 128], P('dp', 'sp', 'sp2')
- w_a: bfloat16 [3, 3, 3, 128, 128], replicated
- bn_a: float32 [3, 2, 128], replicated
- w_down: bfloat16 [3, 3, 128, 256], replicated
- bn_down: float32 [2, 256], replicated
- w_b: bfloat16 [2, 3, 3, 256, 256], replicated
- bn_b: float32 [2, 2, 256], replicated
Outputs:
- output: bfloat16 [8, 32, 256, 256], P('dp', 'sp', 'sp2')
All inputs are finite; a program needn't handle non-finite values.
Results may differ from a plain program's by a relative error of at most 0.00807789.
Values are sent between devices in bfloat16 or wider.
A program may use at most 768 MiB of HBM per device.

v0:
```python
import jax
import jax.numpy as jnp
from jax import lax
from jax.sharding import PartitionSpec as P

CONV_DIMS = ("NHWC", "HWIO", "NHWC")


def edge_extend(act_tile, axis_name, axis_len, line_dim, two_sided):
    tile_len = act_tile.shape[line_dim]
    first_line = lax.slice_in_dim(act_tile, 0, 1, axis=line_dim)
    from_next = lax.ppermute(first_line, axis_name, perm=[(device + 1, device) for device in range(axis_len - 1)])
    if two_sided:
        last_line = lax.slice_in_dim(act_tile, tile_len - 1, tile_len, axis=line_dim)
        from_prev = lax.ppermute(last_line, axis_name, perm=[(device, device + 1) for device in range(axis_len - 1)])
        return jnp.concatenate([from_prev, act_tile, from_next], axis=line_dim)
    return jnp.concatenate([act_tile, from_next], axis=line_dim)


def conv_bn(act_tile, weight, norm_pair, stride, grid_shape):
    rows_n, cols_n = grid_shape
    two_sided = stride == 1
    extended = edge_extend(act_tile, "sp", rows_n, 1, two_sided)
    extended = edge_extend(extended, "sp2", cols_n, 2, two_sided)
    pre_norm = lax.conv_general_dilated(extended, weight, (stride, stride), "VALID", dimension_numbers=CONV_DIMS, preferred_element_type=jnp.float32)
    moments = jnp.stack([jnp.sum(pre_norm, axis=(0, 1, 2)), jnp.sum(pre_norm * pre_norm, axis=(0, 1, 2))])
    moments = lax.psum(moments, ("sp2", "sp"))
    num_pos = pre_norm.shape[0] * pre_norm.shape[1] * pre_norm.shape[2] * rows_n * cols_n
    mean_val = moments[0] / num_pos
    var_val = moments[1] / num_pos - mean_val * mean_val
    normed = norm_pair[0] * (pre_norm - mean_val) * lax.rsqrt(var_val + 1e-5) + norm_pair[1]
    return jnp.maximum(normed, 0.0).astype(jnp.bfloat16)


def solution(mesh):
    grid_shape = (mesh.shape["sp"], mesh.shape["sp2"])

    def per_device(x, w_a, bn_a, w_down, bn_down, w_b, bn_b):
        act_tile = x
        for layer_idx in range(w_a.shape[0]):
            act_tile = conv_bn(act_tile, w_a[layer_idx], bn_a[layer_idx], 1, grid_shape)
        act_tile = conv_bn(act_tile, w_down, bn_down, 2, grid_shape)
        for layer_idx in range(w_b.shape[0]):
            act_tile = conv_bn(act_tile, w_b[layer_idx], bn_b[layer_idx], 1, grid_shape)
        return act_tile

    tile_spec = P("dp", "sp", "sp2", None)
    return jax.shard_map(per_device, mesh=mesh, in_specs=(tile_spec, P(), P(), P(), P(), P(), P()), out_specs=tile_spec, check_vma=False)
```

profile of v0, /device:TPU:97, one launch (start us, length us, event | category | flops | bytes accessed | tf_op | source)
XLA Modules:
  0.0 409.6 jit_solution(10902971069523905160)
XLA Ops:
  1.4 4.6 %collective-permute-start = (bf16[8,1,128,128]{3,0,2,1:T(8,128)(2,1)S(1)}, bf16[8,1,128,128]{3,0,2,1:T(8,128)(2,1)S(1)}, u32[]{:S(2)}, u32[]{:S(2)}) collective-permute-start(bf16[8,1,128,128]{3,0,2,1:T(8,128)(2,1)S(1)} %copy.13), channel_id=1, source_target_pairs={{0,1},{1,2},{2,3},{3,4},{4,5},{5,6},{6,7},{8,9},{9,10},{10,11},{11... | collective-permute-start | bytes 786440 | tf_op jit(solution)/shard_map/ppermute | solution.py:15
  6.2 2.0 collective-permute-start.1
  9.4 1.6 constant_dynamic-update-slice_fusion.1
  10.9 3.0 collective-permute-done.1
  14.0 3.8 collective-permute-start.2
  17.8 1.3 collective-permute-start.3
  19.1 3.6 collective-permute-done.3
  22.7 6.7 %fusion.76 = (f32[128]{0:T(128)S(1)}, f32[128]{0:T(128)S(1)}, f32[8,8,128,128]{3,0,2,1:T(8,128)}) fusion(bf16[3,3,3,128,128]{4,3,2,1,0:T(8,128)(2,1)S(1)} %copy-done.7, bf16[8,10,1,128]{3,0,2,1:T(8,128)(2,1)S(1)} %collective-permute-done.3, bf16[8,10,128,128]{3,0,2,1:T(8,128)(2,1)S(1)} %constant_dynamic-update-slice_fusion, ...), kind=kOutput, calls=%fused_computation.131 | convolution fusion | flops 2421727232 | bytes 7152640 | tf_op jit(solution)/shard_map/conv_general_dilated | solution.py:25
  29.4 45.7 %psum.42 = f32[2,128]{1,0:T(2,128)S(1)} all-reduce(f32[2,128]{1,0:T(2,128)S(1)} %pad_maximum_fusion.16), channel_id=1, replica_groups=mesh['dp'=1,'sp2'=4,'sp'=8] {'sp2','sp'}, use_global_device_ids=true, to_apply=%region_2.0 | all-reduce | flops 256 | bytes 2048 | tf_op jit(solution)/shard_map/psum | solution.py:27
  75.1 3.1 maximum_convert_fusion.2
  78.2 2.3 collective-permute-start.4
  80.5 2.1 collective-permute-start.5
  83.8 4.4 %collective-permute-done.5 = bf16[8,1,128,128]{3,0,2,1:T(8,128)(2,1)S(1)} collective-permute-done((bf16[8,1,128,128]{3,0,2,1:T(8,128)(2,1)S(1)}, bf16[8,1,128,128]{3,0,2,1:T(8,128)(2,1)S(1)}, u32[]{:S(2)}, u32[]{:S(2)}) %collective-permute-start.5) | collective-permute-done | bytes 262176 | tf_op jit(solution)/shard_map/ppermute | solution.py:12
  88.3 2.0 collective-permute-start.6
  91.6 3.2 collective-permute-done.7
  94.8 6.6 %fusion.75 = (f32[128]{0:T(128)S(1)}, f32[128]{0:T(128)S(1)}, f32[8,8,128,128]{3,0,2,1:T(8,128)}) fusion(bf16[3,3,3,128,128]{4,3,2,1,0:T(8,128)(2,1)S(1)} %copy-done.7, bf16[8,10,1,128]{3,0,2,1:T(8,128)(2,1)S(1)} %collective-permute-done.7, bf16[8,1,128,128]{3,0,2,1:T(8,128)(2,1)S(1)} %collective-permute-done.5, ...), kind=kOutput, calls=%fused_computation.130 | convolution fusion | flops 2424389632 | bytes 7152640 | tf_op jit(solution)/shard_map/conv_general_dilated | solution.py:25
  101.5 45.0 %psum.43 = f32[2,128]{1,0:T(2,128)S(1)} all-reduce(f32[2,128]{1,0:T(2,128)S(1)} %pad_maximum_fusion.17), channel_id=1, replica_groups=mesh['dp'=1,'sp2'=4,'sp'=8] {'sp2','sp'}, use_global_device_ids=true, to_apply=%region_5.0 | all-reduce | flops 256 | bytes 2048 | tf_op jit(solution)/shard_map/psum | solution.py:27
  146.5 3.1 maximum_convert_fusion.1
  149.6 2.2 collective-permute-start.8
  151.8 2.2 collective-permute-start.9
  155.1 4.4 %collective-permute-done.9 = bf16[8,1,128,128]{3,0,2,1:T(8,128)(2,1)S(1)} collective-permute-done((bf16[8,1,128,128]{3,0,2,1:T(8,128)(2,1)S(1)}, bf16[8,1,128,128]{3,0,2,1:T(8,128)(2,1)S(1)}, u32[]{:S(2)}, u32[]{:S(2)}) %collective-permute-start.9) | collective-permute-done | bytes 262176 | tf_op jit(solution)/shard_map/ppermute | solution.py:12
  159.6 2.1 collective-permute-start.10
  161.7 1.3 collective-permute-start.11
  163.0 3.2 collective-permute-done.11
  166.3 6.6 %fusion.74 = (f32[128]{0:T(128)S(1)}, f32[128]{0:T(128)S(1)}, f32[8,8,128,128]{3,0,2,1:T(8,128)}) fusion(bf16[3,3,3,128,128]{4,3,2,1,0:T(8,128)(2,1)S(1)} %copy-done.7, bf16[8,10,1,128]{3,0,2,1:T(8,128)(2,1)S(1)} %collective-permute-done.11, bf16[8,1,128,128]{3,0,2,1:T(8,128)(2,1)S(1)} %collective-permute-done.9, ...), kind=kOutput, calls=%fused_computation.129 | convolution fusion | flops 2424389632 | bytes 7152640 | tf_op jit(solution)/shard_map/conv_general_dilated | solution.py:25
  172.9 45.0 %psum.44 = f32[2,128]{1,0:T(2,128)S(1)} all-reduce(f32[2,128]{1,0:T(2,128)S(1)} %pad_maximum_fusion.18), channel_id=1, replica_groups=mesh['dp'=1,'sp2'=4,'sp'=8] {'sp2','sp'}, use_global_device_ids=true, to_apply=%region_8.0 | all-reduce | flops 256 | bytes 2048 | tf_op jit(solution)/shard_map/psum | solution.py:27
  218.0 3.1 maximum_convert_fusion
  221.1 2.9 collective-permute-start.12
  224.0 4.8 %collective-permute-done.12 = bf16[8,1,128,128]{3,0,2,1:T(8,128)(2,1)S(1)} collective-permute-done((bf16[8,1,128,128]{3,0,2,1:T(8,128)(2,1)S(1)}, bf16[8,1,128,128]{3,0,2,1:T(8,128)(2,1)S(1)}, u32[]{:S(2)}, u32[]{:S(2)}) %collective-permute-start.12) | collective-permute-done | bytes 262176 | tf_op jit(solution)/shard_map/ppermute | solution.py:12
  230.1 3.2 collective-permute-done.13
  233.3 1.5 fusion.79
  234.9 43.3 %psum.45 = f32[2,256]{1,0:T(2,128)S(1)} all-reduce(f32[2,256]{1,0:T(2,128)S(1)} %pad_maximum_fusion.13), channel_id=1, replica_groups=mesh['dp'=1,'sp2'=4,'sp'=8] {'sp2','sp'}, use_global_device_ids=true, to_apply=%region_11.0 | all-reduce | flops 512 | bytes 4096 | tf_op jit(solution)/shard_map/psum | solution.py:27
  278.6 2.7 collective-permute-start.14
  281.4 2.0 collective-permute-start.15
  283.3 1.3 collective-permute-done.14
  284.6 4.4 %collective-permute-done.15 = bf16[8,1,64,256]{3,0,2,1:T(8,128)(2,1)S(1)} collective-permute-done((bf16[8,1,64,256]{3,0,2,1:T(8,128)(2,1)S(1)}, bf16[8,1,64,256]{3,0,2,1:T(8,128)(2,1)S(1)}, u32[]{:S(2)}, u32[]{:S(2)}) %collective-permute-start.15) | collective-permute-done | bytes 262176 | tf_op jit(solution)/shard_map/ppermute | solution.py:12
  289.1 1.8 collective-permute-start.16
  290.9 1.5 collective-permute-start.17
  292.4 3.0 collective-permute-done.17
  295.5 2.7 fusion.78
  298.2 44.8 %psum.46 = f32[2,256]{1,0:T(2,128)S(1)} all-reduce(f32[2,256]{1,0:T(2,128)S(1)} %pad_maximum_fusion.14), channel_id=1, replica_groups=mesh['dp'=1,'sp2'=4,'sp'=8] {'sp2','sp'}, use_global_device_ids=true, to_apply=%region_14.0 | all-reduce | flops 512 | bytes 4096 | tf_op jit(solution)/shard_map/psum | solution.py:27
  343.4 2.3 collective-permute-start.18
  345.8 2.2 collective-permute-start.19
  349.0 4.4 %collective-permute-done.19 = bf16[8,1,64,256]{3,0,2,1:T(8,128)(2,1)S(1)} collective-permute-done((bf16[8,1,64,256]{3,0,2,1:T(8,128)(2,1)S(1)}, bf16[8,1,64,256]{3,0,2,1:T(8,128)(2,1)S(1)}, u32[]{:S(2)}, u32[]{:S(2)}) %collective-permute-start.19) | collective-permute-done | bytes 262176 | tf_op jit(solution)/shard_map/ppermute | solution.py:12
  353.5 2.2 collective-permute-start.20
  357.0 3.3 collective-permute-done.21
  360.3 2.7 fusion.77
  363.0 45.0 %psum.47 = f32[2,256]{1,0:T(2,128)S(1)} all-reduce(f32[2,256]{1,0:T(2,128)S(1)} %pad_maximum_fusion.15), channel_id=1, replica_groups=mesh['dp'=1,'sp2'=4,'sp'=8] {'sp2','sp'}, use_global_device_ids=true, to_apply=%region_17.0 | all-reduce | flops 512 | bytes 4096 | tf_op jit(solution)/shard_map/psum | solution.py:27
  (69 shorter events, 12.8 us)
Async XLA Ops:
  0.0 233.3 %copy-start = (bf16[3,3,128,256]{3,2,1,0:T(8,128)(2,1)S(1)}, bf16[3,3,128,256]{3,2,1,0:T(8,128)(2,1)}, u32[]{:S(2)}) copy-start(bf16[3,3,128,256]{3,2,1,0:T(8,128)(2,1)} %param.10) | copy-start | bytes 1769476
  0.0 9.3 %copy-start.1 = (bf16[8,8,128,128]{3,2,1,0:T(8,128)(2,1)S(1)}, bf16[8,8,128,128]{3,2,1,0:T(8,128)(2,1)}, u32[]{:S(2)}) copy-start(bf16[8,8,128,128]{3,2,1,0:T(8,128)(2,1)} %param.7) | copy-start | bytes 6291460
  1.4 7.9 %collective-permute-start = (bf16[8,1,128,128]{3,0,2,1:T(8,128)(2,1)S(1)}, bf16[8,1,128,128]{3,0,2,1:T(8,128)(2,1)S(1)}, u32[]{:S(2)}, u32[]{:S(2)}) collective-permute-start(bf16[8,1,128,128]{3,0,2,1:T(8,128)(2,1)S(1)} %copy.13), channel_id=1, source_target_pairs={{0,1},{1,2},{2,3},{3,4},{4,5},{5,6},{6,7},{8,9},{9,10},{10,11},{11... | collective-permute-start | bytes 786440 | tf_op jit(solution)/shard_map/ppermute | solution.py:15
  6.2 7.7 %collective-permute-start.1 = (bf16[8,1,128,128]{3,0,2,1:T(8,128)(2,1)S(1)}, bf16[8,1,128,128]{3,0,2,1:T(8,128)(2,1)S(1)}, u32[]{:S(2)}, u32[]{:S(2)}) collective-permute-start(bf16[8,1,128,128]{3,0,2,1:T(8,128)(2,1)S(1)} %copy.14), channel_id=1, source_target_pairs={{1,0},{2,1},{3,2},{4,3},{5,4},{6,5},{7,6},{9,8},{10,9},{11,10},{12... | collective-permute-start | bytes 786440 | tf_op jit(solution)/shard_map/ppermute | solution.py:12
  9.3 9.8 %copy-start.3 = (f32[3,2,128]{2,1,0:T(2,128)S(1)}, f32[3,2,128]{2,1,0:T(2,128)}, u32[]{:S(2)}) copy-start(f32[3,2,128]{2,1,0:T(2,128)} %param.9) | copy-start | bytes 9220
  9.3 13.4 %copy-start.7 = (bf16[3,3,3,128,128]{4,3,2,1,0:T(8,128)(2,1)S(1)}, bf16[3,3,3,128,128]{4,3,2,1,0:T(8,128)(2,1)}, u32[]{:S(2)}) copy-start(bf16[3,3,3,128,128]{4,3,2,1,0:T(8,128)(2,1)} %param.8) | copy-start | bytes 2654212
  14.0 5.1 %collective-permute-start.2 = (bf16[8,10,1,128]{3,0,2,1:T(8,128)(2,1)S(1)}, bf16[8,10,1,128]{3,0,2,1:T(8,128)(2,1)S(1)}, u32[]{:S(2)}, u32[]{:S(2)}) collective-permute-start(bf16[8,10,1,128]{3,0,2,1:T(8,128)(2,1)S(1)} %get-tuple-element.21), channel_id=1, source_target_pairs={{0,8},{8,16},{16,24},{1,9},{9,17},{17,25},{2,10},{10,18},{18,26},{... | collective-permute-start | bytes 61448 | tf_op jit(solution)/shard_map/ppermute | solution.py:15
  17.8 4.9 %collective-permute-start.3 = (bf16[8,10,1,128]{3,0,2,1:T(8,128)(2,1)S(1)}, bf16[8,10,1,128]{3,0,2,1:T(8,128)(2,1)S(1)}, u32[]{:S(2)}, u32[]{:S(2)}) collective-permute-start(bf16[8,10,1,128]{3,0,2,1:T(8,128)(2,1)S(1)} %get-tuple-element.22), channel_id=1, source_target_pairs={{8,0},{16,8},{24,16},{9,1},{17,9},{25,17},{10,2},{18,10},{26,18},{... | collective-permute-start | bytes 61448 | tf_op jit(solution)/shard_map/ppermute | solution.py:12
  78.2 5.6 %collective-permute-start.4 = (bf16[8,1,128,128]{3,0,2,1:T(8,128)(2,1)S(1)}, bf16[8,1,128,128]{3,0,2,1:T(8,128)(2,1)S(1)}, u32[]{:S(2)}, u32[]{:S(2)}) collective-permute-start(bf16[8,1,128,128]{3,0,2,1:T(8,128)(2,1)S(1)} %get-tuple-element.25), channel_id=1, source_target_pairs={{0,1},{1,2},{2,3},{3,4},{4,5},{5,6},{6,7},{8,9},{9,10},{10,11},{11... | collective-permute-start | bytes 786440 | tf_op jit(solution)/shard_map/ppermute | solution.py:15
  80.5 7.7 %collective-permute-start.5 = (bf16[8,1,128,128]{3,0,2,1:T(8,128)(2,1)S(1)}, bf16[8,1,128,128]{3,0,2,1:T(8,128)(2,1)S(1)}, u32[]{:S(2)}, u32[]{:S(2)}) collective-permute-start(bf16[8,1,128,128]{3,0,2,1:T(8,128)(2,1)S(1)} %get-tuple-element.26), channel_id=1, source_target_pairs={{1,0},{2,1},{3,2},{4,3},{5,4},{6,5},{7,6},{9,8},{10,9},{11,10},{12... | collective-permute-start | bytes 786440 | tf_op jit(solution)/shard_map/ppermute | solution.py:12
  88.3 3.3 collective-permute-start.6
  90.3 4.6 %collective-permute-start.7 = (bf16[8,10,1,128]{3,0,2,1:T(8,128)(2,1)S(1)}, bf16[8,10,1,128]{3,0,2,1:T(8,128)(2,1)S(1)}, u32[]{:S(2)}, u32[]{:S(2)}) collective-permute-start(bf16[8,10,1,128]{3,0,2,1:T(8,128)(2,1)S(1)} %get-tuple-element.20), channel_id=1, source_target_pairs={{8,0},{16,8},{24,16},{9,1},{17,9},{25,17},{10,2},{18,10},{26,18},{... | collective-permute-start | bytes 61448 | tf_op jit(solution)/shard_map/ppermute | solution.py:12
  149.6 5.5 %collective-permute-start.8 = (bf16[8,1,128,128]{3,0,2,1:T(8,128)(2,1)S(1)}, bf16[8,1,128,128]{3,0,2,1:T(8,128)(2,1)S(1)}, u32[]{:S(2)}, u32[]{:S(2)}) collective-permute-start(bf16[8,1,128,128]{3,0,2,1:T(8,128)(2,1)S(1)} %get-tuple-element.23), channel_id=1, source_target_pairs={{0,1},{1,2},{2,3},{3,4},{4,5},{5,6},{6,7},{8,9},{9,10},{10,11},{11... | collective-permute-start | bytes 786440 | tf_op jit(solution)/shard_map/ppermute | solution.py:15
  151.8 7.7 %collective-permute-start.9 = (bf16[8,1,128,128]{3,0,2,1:T(8,128)(2,1)S(1)}, bf16[8,1,128,128]{3,0,2,1:T(8,128)(2,1)S(1)}, u32[]{:S(2)}, u32[]{:S(2)}) collective-permute-start(bf16[8,1,128,128]{3,0,2,1:T(8,128)(2,1)S(1)} %get-tuple-element.24), channel_id=1, source_target_pairs={{1,0},{2,1},{3,2},{4,3},{5,4},{6,5},{7,6},{9,8},{10,9},{11,10},{12... | collective-permute-start | bytes 786440 | tf_op jit(solution)/shard_map/ppermute | solution.py:12
  159.6 3.5 collective-permute-start.10
  161.7 4.6 %collective-permute-start.11 = (bf16[8,10,1,128]{3,0,2,1:T(8,128)(2,1)S(1)}, bf16[8,10,1,128]{3,0,2,1:T(8,128)(2,1)S(1)}, u32[]{:S(2)}, u32[]{:S(2)}) collective-permute-start(bf16[8,10,1,128]{3,0,2,1:T(8,128)(2,1)S(1)} %get-tuple-element.18), channel_id=1, source_target_pairs={{8,0},{16,8},{24,16},{9,1},{17,9},{25,17},{10,2},{18,10},{26,18},{... | collective-permute-start | bytes 61448 | tf_op jit(solution)/shard_map/ppermute | solution.py:12
  221.0 9.1 %copy-start.4 = (f32[2,256]{1,0:T(2,128)S(1)}, f32[2,256]{1,0:T(2,128)}, u32[]{:S(2)}) copy-start(f32[2,256]{1,0:T(2,128)} %param.11) | copy-start | bytes 6148
  221.1 7.7 %collective-permute-start.12 = (bf16[8,1,128,128]{3,0,2,1:T(8,128)(2,1)S(1)}, bf16[8,1,128,128]{3,0,2,1:T(8,128)(2,1)S(1)}, u32[]{:S(2)}, u32[]{:S(2)}) collective-permute-start(bf16[8,1,128,128]{3,0,2,1:T(8,128)(2,1)S(1)} %slice.237), channel_id=1, source_target_pairs={{1,0},{2,1},{3,2},{4,3},{5,4},{6,5},{7,6},{9,8},{10,9},{11,10},{12... | collective-permute-start | bytes 786440 | tf_op jit(solution)/shard_map/ppermute | solution.py:12
  228.8 4.5 %collective-permute-start.13 = (bf16[8,9,1,128]{3,0,2,1:T(8,128)(2,1)S(1)}, bf16[8,9,1,128]{3,0,2,1:T(8,128)(2,1)S(1)}, u32[]{:S(2)}, u32[]{:S(2)}) collective-permute-start(bf16[8,9,1,128]{3,0,2,1:T(8,128)(2,1)S(1)} %pad_maximum_fusion.12), channel_id=1, source_target_pairs={{8,0},{16,8},{24,16},{9,1},{17,9},{25,17},{10,2},{18,10},{26,18},{... | collective-permute-start | bytes 55304 | tf_op jit(solution)/shard_map/ppermute | solution.py:12
  278.2 14.2 %copy-start.2 = (f32[2,2,256]{2,1,0:T(2,128)S(1)}, f32[2,2,256]{2,1,0:T(2,128)}, u32[]{:S(2)}) copy-start(f32[2,2,256]{2,1,0:T(2,128)} %param.13) | copy-start | bytes 12292
  278.2 17.3 %copy-start.5 = (bf16[2,3,3,256,256]{4,3,2,1,0:T(8,128)(2,1)S(1)}, bf16[2,3,3,256,256]{4,3,2,1,0:T(8,128)(2,1)}, u32[]{:S(2)}) copy-start(bf16[2,3,3,256,256]{4,3,2,1,0:T(8,128)(2,1)} %param.12) | copy-start | bytes 7077892
  278.6 6.0 %collective-permute-start.14 = (bf16[8,1,64,256]{3,0,2,1:T(8,128)(2,1)S(1)}, bf16[8,1,64,256]{3,0,2,1:T(8,128)(2,1)S(1)}, u32[]{:S(2)}, u32[]{:S(2)}) collective-permute-start(bf16[8,1,64,256]{3,0,2,1:T(8,128)(2,1)S(1)} %get-tuple-element.35), channel_id=1, source_target_pairs={{0,1},{1,2},{2,3},{3,4},{4,5},{5,6},{6,7},{8,9},{9,10},{10,11},{11... | collective-permute-start | bytes 786440 | tf_op jit(solution)/shard_map/ppermute | solution.py:15
  281.4 7.7 %collective-permute-start.15 = (bf16[8,1,64,256]{3,0,2,1:T(8,128)(2,1)S(1)}, bf16[8,1,64,256]{3,0,2,1:T(8,128)(2,1)S(1)}, u32[]{:S(2)}, u32[]{:S(2)}) collective-permute-start(bf16[8,1,64,256]{3,0,2,1:T(8,128)(2,1)S(1)} %get-tuple-element.36), channel_id=1, source_target_pairs={{1,0},{2,1},{3,2},{4,3},{5,4},{6,5},{7,6},{9,8},{10,9},{11,10},{12... | collective-permute-start | bytes 786440 | tf_op jit(solution)/shard_map/ppermute | solution.py:12
  289.1 3.3 collective-permute-start.16
  290.9 4.6 %collective-permute-start.17 = (bf16[8,6,1,256]{3,0,2,1:T(8,128)(2,1)S(1)}, bf16[8,6,1,256]{3,0,2,1:T(8,128)(2,1)S(1)}, u32[]{:S(2)}, u32[]{:S(2)}) collective-permute-start(bf16[8,6,1,256]{3,0,2,1:T(8,128)(2,1)S(1)} %get-tuple-element.32), channel_id=1, source_target_pairs={{8,0},{16,8},{24,16},{9,1},{17,9},{25,17},{10,2},{18,10},{26,18},{... | collective-permute-start | bytes 73736 | tf_op jit(solution)/shard_map/ppermute | solution.py:12
  343.0 17.3 %copy-start.6 = (bf16[2,3,3,256,256]{4,3,2,1,0:T(8,128)(2,1)S(1)}, bf16[2,3,3,256,256]{4,3,2,1,0:T(8,128)(2,1)}, u32[]{:S(2)}) copy-start(bf16[2,3,3,256,256]{4,3,2,1,0:T(8,128)(2,1)} %param.12) | copy-start | bytes 7077892
  343.4 5.6 %collective-permute-start.18 = (bf16[8,1,64,256]{3,0,2,1:T(8,128)(2,1)S(1)}, bf16[8,1,64,256]{3,0,2,1:T(8,128)(2,1)S(1)}, u32[]{:S(2)}, u32[]{:S(2)}) collective-permute-start(bf16[8,1,64,256]{3,0,2,1:T(8,128)(2,1)S(1)} %get-tuple-element.33), channel_id=1, source_target_pairs={{0,1},{1,2},{2,3},{3,4},{4,5},{5,6},{6,7},{8,9},{9,10},{10,11},{11... | collective-permute-start | bytes 786440 | tf_op jit(solution)/shard_map/ppermute | solution.py:15
  345.8 7.7 %collective-permute-start.19 = (bf16[8,1,64,256]{3,0,2,1:T(8,128)(2,1)S(1)}, bf16[8,1,64,256]{3,0,2,1:T(8,128)(2,1)S(1)}, u32[]{:S(2)}, u32[]{:S(2)}) collective-permute-start(bf16[8,1,64,256]{3,0,2,1:T(8,128)(2,1)S(1)} %get-tuple-element.34), channel_id=1, source_target_pairs={{1,0},{2,1},{3,2},{4,3},{5,4},{6,5},{7,6},{9,8},{10,9},{11,10},{12... | collective-permute-start | bytes 786440 | tf_op jit(solution)/shard_map/ppermute | solution.py:12
  353.5 3.5 collective-permute-start.20
  355.7 4.6 %collective-permute-start.21 = (bf16[8,6,1,256]{3,0,2,1:T(8,128)(2,1)S(1)}, bf16[8,6,1,256]{3,0,2,1:T(8,128)(2,1)S(1)}, u32[]{:S(2)}, u32[]{:S(2)}) collective-permute-start(bf16[8,6,1,256]{3,0,2,1:T(8,128)(2,1)S(1)} %get-tuple-element.30), channel_id=1, source_target_pairs={{8,0},{16,8},{24,16},{9,1},{17,9},{25,17},{10,2},{18,10},{26,18},{... | collective-permute-start | bytes 73736 | tf_op jit(solution)/shard_map/ppermute | solution.py:12
where the time goes:
time: 411 us; the launch traced here: 410 us
  blocking collectives  269 us (65%)
  waiting for transfers between devices  50.9 us (12%)
  starting transfers between devices  47.4 us (12%)
  matrix products  26.9 us (7%)
  other arithmetic  10.5 us (3%)
  local copies, waits for them, and re-layouts  4.62 us (1%)
    psum x6, blocking collectives, conv_bn(): moments = lax.psum(moments, ('sp2', 'sp'))  269 us
    ppermute x12, waiting for transfers between devices, edge_extend(): lax.ppermute(first_line, axis_name, perm=[(device + 1, device) for device...  45.2 us
    conv_general_dilated x6, matrix products, conv_bn(): lax.conv_general_dilated(extended, weight, (stride, stride), 'VALID', dim...  26.9 us
    ppermute x10, starting transfers between devices, edge_extend(): lax.ppermute(last_line, axis_name, perm=[(device, device + 1) for device...  26 us
    ppermute x12, starting transfers between devices, edge_extend(): lax.ppermute(first_line, axis_name, perm=[(device + 1, device) for device...  21.4 us
    convert_element_type x6, other arithmetic, conv_bn(): return jnp.maximum(normed, 0.0).astype(jnp.bfloat16)  10.4 us
  transfers between devices with their start and end apart: 22, of which 17 were waited for; matrix products, arithmetic and copies ran while one was open for 0% of the time, Pallas kernels for 0%

commit v1 on v0

v1 whole, which is shorter than its diff:
```python
import functools

import jax
import jax.numpy as jnp
from jax import lax
from jax.experimental import pallas as pl
from jax.experimental.pallas import tpu as pltpu
from jax.sharding import PartitionSpec as P

MESH = pl.DeviceIdType.MESH
F32 = jnp.float32
BF16 = jnp.bfloat16
EPS = 1e-5
PAD = 8


def net_kernel(dims, x, w_a, bn_a, w_down, bn_down, w_b, bn_b, y,
               xin, xh, xf, za, zb, ha, hb, yfa, yfb, ya, sa, yb,
               cs, cl, ksa, kla, ksb, klb, ta, tb, wy, ws, wd, wb, ga, gd, gb, yo,
               in_sem, w_sem, row_recv, row_send, col_recv, col_send, cor_recv, cor_send, st_recv, st_send, out_sem):
    rows_n, cols_n, n_img, height, width, chan = dims
    n_dev = rows_n * cols_n
    half_w = width // 2
    low_h = height // 2
    xstride = width + 2 * PAD
    fstride = half_w + 2 * PAD
    sp = lax.axis_index("sp")
    sp2 = lax.axis_index("sp2")
    me = sp2 * rows_n + sp
    has_up = sp > 0
    has_down = sp < rows_n - 1
    has_left = sp2 > 0
    has_right = sp2 < cols_n - 1
    row_ok = (has_up, has_down)
    col_ok = (has_left, has_right)
    cor_ok = tuple(r & c for r in row_ok for c in col_ok)

    def device(d_sp, d_sp2):
        return {"sp": sp + d_sp, "sp2": sp2 + d_sp2}

    for i in range(n_img):
        pltpu.make_async_copy(x.at[i], xin.at[i], in_sem.at[i]).start()
    weight_copies = []
    for kx, dst, k0, n0 in ((1, wy, 0, 0), (1, wy, chan, chan), (0, wy, 0, chan), (2, wy, chan, 0), (0, ws, 0, 0), (2, ws, chan, chan)):
        weight_copies.append((w_a.at[:, :, kx], dst.at[:, :, pl.ds(k0, chan), pl.ds(n0, chan)]))
    weight_copies.append((w_down.at[:, 0], wd.at[:, 0, pl.ds(0, chan), :]))
    weight_copies.append((w_down.at[:, 1], wd.at[:, 0, pl.ds(chan, chan), :]))
    weight_copies.append((w_down.at[:, 2], wd.at[:, 1, pl.ds(chan, chan), :]))
    weight_copies.append((w_b, wb))
    weight_copies.append((bn_a, ga))
    weight_copies.append((bn_down, gd))
    weight_copies.append((bn_b, gb))
    weight_copies = [pltpu.make_async_copy(s, d, w_sem.at[k]) for k, (s, d) in enumerate(weight_copies)]
    for copy in weight_copies:
        copy.start()

    barrier = pltpu.get_barrier_semaphore()

    def to_device(index):
        return {"sp": lax.rem(index, rows_n), "sp2": lax.div(index, rows_n)}

    def greet(k, carry):
        pl.semaphore_signal(barrier, inc=1, device_id=to_device(lax.rem(me + k, n_dev)), device_id_type=MESH)
        return carry

    lax.fori_loop(1, n_dev, greet, 0)

    zeros = jnp.zeros((chan, chan), BF16)
    for layer in range(3):
        for ky in range(3):
            ws[layer, ky, 0:chan, chan:2 * chan] = zeros
            ws[layer, ky, chan:2 * chan, 0:chan] = zeros
    for ky in range(3):
        wd[ky, 1, 0:chan, :] = jnp.zeros((chan, 2 * chan), BF16)

    for i in range(n_img):
        pltpu.make_async_copy(x.at[i], xin.at[i], in_sem.at[i]).wait()
    for i in range(n_img):
        for side, col0, line in ((0, 0, 0), (1, width - 16, 15)):
            blk = xin[i, :, col0:col0 + 16, :].astype(F32)
            yfa[0:height * 16, :] = blk.reshape(height * 16, chan)
            edge = yfa[pl.ds(line, height, stride=16), :]
            cs[0, side, i] = edge
            ksa[0, side, i] = edge[0:1]
            ksa[0, 2 + side, i] = edge[height - 1:height]

    pl.semaphore_wait(barrier, n_dev - 1)

    def cor_bufs(e):
        return (ksa.at[e], kla.at[e]) if e < 4 else (ksb.at[e - 4], klb.at[e - 4])

    def start_cols(e, sides=(0, 1), corners=(0, 1, 2, 3)):
        for side in sides:
            d = -1 if side == 0 else 1

            @pl.when(col_ok[side])
            def _():
                pltpu.make_async_remote_copy(cs.at[e, side], cl.at[e, 1 - side], col_send.at[e, side], col_recv.at[e, 1 - side],
                                             device_id=device(0, d), device_id_type=MESH).start()
        src, dst = cor_bufs(e)
        for corner in corners:
            d_sp = -1 if corner < 2 else 1
            d_sp2 = -1 if corner % 2 == 0 else 1

            @pl.when(cor_ok[corner])
            def _():
                pltpu.make_async_remote_copy(src.at[corner], dst.at[3 - corner], cor_send.at[e, corner], cor_recv.at[e, 3 - corner],
                                             device_id=device(d_sp, d_sp2), device_id_type=MESH).start()

    def wait_cols(e, sides=(0, 1), corners=(0, 1, 2, 3)):
        for side in sides:
            @pl.when(col_ok[side])
            def _():
                pltpu.make_async_copy(cl.at[e, side], cl.at[e, side], col_recv.at[e, side]).wait()
        src, dst = cor_bufs(e)
        for corner in corners:
            @pl.when(cor_ok[corner])
            def _():
                pltpu.make_async_copy(dst.at[corner], dst.at[corner], cor_recv.at[e, corner]).wait()

    def wait_col_sends(e, sides=(0, 1), corners=(0, 1, 2, 3)):
        for side in sides:
            @pl.when(col_ok[side])
            def _():
                pltpu.make_async_copy(cs.at[e, side], cs.at[e, side], col_send.at[e, side]).wait()
        src, dst = cor_bufs(e)
        for corner in corners:
            @pl.when(cor_ok[corner])
            def _():
                pltpu.make_async_copy(src.at[corner], src.at[corner], cor_send.at[e, corner]).wait()

    def row_landing(e, side):
        if e == 0:
            return xh.at[side]
        return ha.at[e - 1, side] if e < 4 else hb.at[e - 4, side]

    def send_row(e, side, i, src):
        @pl.when(row_ok[side])
        def _():
            pltpu.make_async_remote_copy(src, row_landing(e, 1 - side).at[i], row_send.at[e, side, i], row_recv.at[e, 1 - side, i],
                                         device_id=device(-1 if side == 0 else 1, 0), device_id_type=MESH).start()

    def wait_row(e, side, i):
        @pl.when(row_ok[side])
        def _():
            ref = row_landing(e, side).at[i]
            pltpu.make_async_copy(ref, ref, row_recv.at[e, side, i]).wait()

    def wait_row_sends(e, sides=(0, 1)):
        for side in sides:
            @pl.when(row_ok[side])
            def _():
                ref = row_landing(e, side)

                def one(i, carry):
                    pltpu.make_async_copy(ref.at[i], ref.at[i], row_send.at[e, side, i]).wait()
                    return carry

                lax.fori_loop(0, n_img, one, 0)

    def sums_refs(e):
        return ta.at[e] if e < 3 else tb.at[e - 3]

    def start_sums(e, part):
        buf = sums_refs(e)
        buf[me] = part

        def send(k, carry):
            to = to_device(lax.rem(me + k, n_dev))
            pltpu.make_async_remote_copy(buf.at[me], buf.at[me], st_send.at[e], st_recv.at[e], device_id=to, device_id_type=MESH).start()
            return carry

        lax.fori_loop(1, n_dev, send, 0)

    def finish_sums(e, num_pos):
        buf = sums_refs(e)
        rest = buf.at[pl.ds(0, n_dev - 1)]
        pltpu.make_async_copy(rest, rest, st_recv.at[e]).wait()
        total = jnp.sum(buf[...], axis=0) / num_pos
        lines = total.shape[0] // 2
        mean = total[0:lines]
        var = total[lines:] - mean * mean
        return mean, lax.rsqrt(var + EPS)

    def bn(z, par):
        mean, inv, gain, shift = par
        return jnp.maximum(gain * (z - mean) * inv + shift, 0.0)

    def keep(cond, val):
        return jnp.where(cond, val, 0.0)

    def prep_x(i):
        for side in range(2):
            wait_row(0, side, i)
        last = height + 1
        for r in range(height):
            xf[pl.ds((r + 1) * xstride + PAD, width), :] = xin[i, r].astype(F32)
        xf[pl.ds(PAD, width), :] = keep(has_up, xh[0, i].astype(F32))
        xf[pl.ds(last * xstride + PAD, width), :] = keep(has_down, xh[1, i].astype(F32))
        xf[pl.ds(xstride + PAD - 1, height, stride=xstride), :] = keep(has_left, cl[0, 0, i])
        xf[pl.ds(xstride + PAD + width, height, stride=xstride), :] = keep(has_right, cl[0, 1, i])
        for corner in range(4):
            row = 0 if corner < 2 else last
            col = PAD - 1 if corner % 2 == 0 else PAD + width
            xf[row * xstride + col:row * xstride + col + 1, :] = keep(cor_ok[corner], kla[0, corner, i])
        for r in range(height + 2):
            base = r * xstride + PAD
            even = xf[pl.ds(base, half_w, stride=2), :]
            odd = xf[pl.ds(base + 1, half_w, stride=2), :]
            before = xf[pl.ds(base - 1, half_w, stride=2), :]
            after = xf[pl.ds(base + 2, half_w, stride=2), :]
            ya[r] = jnp.concatenate([even, odd], axis=1).astype(BF16)
            sa[r] = jnp.concatenate([before, after], axis=1).astype(BF16)

    def norm_a(e, slot, par, i, up=True):
        last = height + 1
        lo = 0 if up else 1
        for side in (0, 1) if up else (1,):
            wait_row(e, side, i)
        for r in range(lo, height + 2):
            if r == 0:
                val = keep(has_up, bn(ha[e - 1, 0, i], par))
            elif r == last:
                val = keep(has_down, bn(ha[e - 1, 1, i], par))
            else:
                val = bn(za[slot, i, pl.ds((r - 1) * 2 * half_w, 2 * half_w), :], par)
            base = r * 2 * fstride + PAD
            yfa[base:base + half_w, :] = val[0:half_w]
            yfa[base + fstride:base + fstride + half_w, :] = val[half_w:]
        if up:
            yfa[pl.ds(3 * fstride + PAD - 1, height, stride=2 * fstride), :] = keep(has_left, bn(cl[e, 0, i], par))
        yfa[pl.ds(2 * fstride + PAD + half_w, height, stride=2 * fstride), :] = keep(has_right, bn(cl[e, 1, i], par))
        for corner in range(4) if up else (3,):
            row = 0 if corner < 2 else last
            at = row * 2 * fstride + (fstride + PAD - 1 if corner % 2 == 0 else PAD + half_w)
            yfa[at:at + 1, :] = keep(cor_ok[corner], bn(kla[e, corner, i], par))
        for r in range(lo, height + 2):
            base = r * 2 * fstride + PAD
            even = yfa[base:base + half_w, :]
            odd = yfa[base + fstride:base + fstride + half_w, :]
            before = yfa[base + fstride - 1:base + fstride - 1 + half_w, :]
            after = yfa[base + 1:base + 1 + half_w, :]
            ya[r] = jnp.concatenate([even, odd], axis=1).astype(BF16)
            sa[r] = jnp.concatenate([before, after], axis=1).astype(BF16)

    def norm_b(e, slot, par, i):
        last = low_h + 1
        halves = [tuple(p[h:h + 1] for p in par) for h in range(2)]
        tall = tuple(jnp.concatenate([p] * low_h, axis=0) for p in par)
        for side in range(2):
            wait_row(e, side, i)
        for r in range(low_h + 2):
            for h in range(2):
                if r == 0:
                    val = keep(has_up, bn(hb[e - 4, 0, i, pl.ds(h * half_w, half_w), :], halves[h]))
                elif r == last:
                    val = keep(has_down, bn(hb[e - 4, 1, i, pl.ds(h * half_w, half_w), :], halves[h]))
                else:
                    val = bn(zb[slot, i, pl.ds(((r - 1) * 2 + h) * half_w, half_w), :], halves[h])
                base = (r * 2 + h) * fstride + PAD
                yfb[base:base + half_w, :] = val
        yfb[pl.ds(2 * fstride + PAD - 1, 2 * low_h, stride=fstride), :] = keep(has_left, bn(cl[e, 0, i], tall))
        yfb[pl.ds(2 * fstride + PAD + half_w, 2 * low_h, stride=fstride), :] = keep(has_right, bn(cl[e, 1, i], tall))
        for corner in range(4):
            row = 0 if corner < 2 else last
            val = keep(cor_ok[corner], bn(klb[e - 4, corner, i], par))
            for h in range(2):
                at = (row * 2 + h) * fstride + (PAD - 1 if corner % 2 == 0 else PAD + half_w)
                yfb[at:at + 1, :] = val[h:h + 1]
        for r in range(low_h + 2):
            base = r * 2 * fstride + PAD
            for kx in range(3):
                at = base + kx - 1
                yb[kx, r] = jnp.concatenate([yfb[at:at + half_w, :], yfb[at + fstride:at + fstride + half_w, :]], axis=1).astype(BF16)

    def add_sums(acc, carry):
        tiles = acc.reshape(acc.shape[0] // 8, 8, acc.shape[1])
        return carry[0] + jnp.sum(tiles, axis=0), carry[1] + jnp.sum(tiles * tiles, axis=0)

    zero_sums = (jnp.zeros((8, 2 * chan), F32), jnp.zeros((8, 2 * chan), F32))

    def edges_a(e, slot, i, rows=(0, 1)):
        first = za[slot, i, pl.ds(0, height, stride=2 * half_w), :]
        final = za[slot, i, pl.ds(2 * half_w - 1, height, stride=2 * half_w), :]
        for side, edge in enumerate((first, final)):
            cs[e, side, i] = edge
            ksa[e, side, i] = edge[0:1]
            ksa[e, 2 + side, i] = edge[height - 1:height]
        for side in rows:
            at = 0 if side == 0 else (height - 1) * 2 * half_w
            send_row(e, side, i, za.at[slot, i, pl.ds(at, 2 * half_w), :])

    def edges_b(e, slot, i):
        first = zb[slot, i, pl.ds(0, 2 * low_h, stride=half_w), :]
        final = zb[slot, i, pl.ds(half_w - 1, 2 * low_h, stride=half_w), :]
        for side, edge in enumerate((first, final)):
            cs[e, side, i] = edge
            ksb[e - 4, side, i] = edge[0:2]
            ksb[e - 4, 2 + side, i] = edge[2 * low_h - 2:2 * low_h]
        for side in range(2):
            at = 0 if side == 0 else (low_h - 1) * 2 * half_w
            send_row(e, side, i, zb.at[slot, i, pl.ds(at, 2 * half_w), :])

    def store_z(ref, slot, i, acc, rows):
        for r in range(rows):
            at = r * 2 * half_w
            ref[slot, i, at:at + half_w, :] = acc[r * half_w:(r + 1) * half_w, 0:chan]
            ref[slot, i, at + half_w:at + 2 * half_w, :] = acc[r * half_w:(r + 1) * half_w, chan:2 * chan]

    def layer_a(layer, prep, rows):
        e, slot = layer + 1, layer % 2

        def image(i, carry):
            prep(i)
            acc = None
            for ky in range(3):
                for ref, w in ((ya, wy), (sa, ws)):
                    lhs = ref[ky:ky + height].reshape(height * half_w, 2 * chan)
                    d = jnp.dot(lhs, w[layer, ky], preferred_element_type=F32)
                    acc = d if acc is None else acc + d
            store_z(za, slot, i, acc, height)
            edges_a(e, slot, i, rows)
            return add_sums(acc, carry)

        s1, s2 = lax.fori_loop(0, n_img, image, zero_sums)
        s1, s2 = (jnp.sum(s, axis=0, keepdims=True) for s in (s1, s2))
        return jnp.concatenate([s1[:, 0:chan] + s1[:, chan:], s2[:, 0:chan] + s2[:, chan:]], axis=0)

    def layer_down(prep):
        def image(i, carry):
            prep(i)
            acc = None
            for ky in range(3):
                for part, ref in enumerate((ya, sa)):
                    lhs = jnp.concatenate([ref[1 + 2 * r + ky] for r in range(low_h)], axis=0)
                    d = jnp.dot(lhs, wd[ky, part], preferred_element_type=F32)
                    acc = d if acc is None else acc + d
            store_z(zb, 0, i, acc, low_h)
            edges_b(4, 0, i)
            return add_sums(acc, carry)

        return wide_part(lax.fori_loop(0, n_img, image, zero_sums))

    def wide_part(sums):
        s1, s2 = (jnp.sum(s, axis=0, keepdims=True) for s in sums)
        return jnp.concatenate([s1[:, 0:chan], s1[:, chan:], s2[:, 0:chan], s2[:, chan:]], axis=0)

    def layer_b(layer, prep, edges):
        slot = (layer + 1) % 2

        def image(i, carry):
            prep(i)
            acc = None
            for ky in range(3):
                for kx in range(3):
                    lhs = yb[kx, ky:ky + low_h].reshape(low_h * half_w, 2 * chan)
                    d = jnp.dot(lhs, wb[layer, ky, kx], preferred_element_type=F32)
                    acc = d if acc is None else acc + d
            store_z(zb, slot, i, acc, low_h)
            if edges:
                edges_b(5 + layer, slot, i)
            return add_sums(acc, carry)

        return wide_part(lax.fori_loop(0, n_img, image, zero_sums))

    for side in range(2):
        def send_x(i, carry, side=side):
            send_row(0, side, i, xin.at[i, 0 if side == 0 else height - 1])
            return carry

        lax.fori_loop(0, n_img, send_x, 0)
    start_cols(0)
    for copy in weight_copies:
        copy.wait()
    wait_cols(0)

    pos_a = n_dev * n_img * height * width
    pos_b = n_dev * n_img * low_h * half_w

    def params_a(e, layer):
        mean, inv = finish_sums(e, pos_a)
        return mean, inv, ga[layer, 0:1], ga[layer, 1:2]

    def params_b(e, ref):
        mean, inv = finish_sums(e, pos_b)
        gain = jnp.concatenate([ref[0:1, 0:chan], ref[0:1, chan:]], axis=0)
        shift = jnp.concatenate([ref[1:2, 0:chan], ref[1:2, chan:]], axis=0)
        return mean, inv, gain, shift

    start_sums(0, layer_a(0, prep_x, (0, 1)))
    start_cols(1)

    wait_row_sends(0)
    wait_col_sends(0)
    wait_cols(1)
    par = params_a(0, 0)
    start_sums(1, layer_a(1, functools.partial(norm_a, 1, 0, par), (0, 1)))
    start_cols(2)

    wait_row_sends(1)
    wait_col_sends(1)
    wait_cols(2)
    par = params_a(1, 1)
    start_sums(2, layer_a(2, functools.partial(norm_a, 2, 1, par), (0,)))
    start_cols(3, (0,), (0,))

    wait_row_sends(2)
    wait_col_sends(2)
    wait_cols(3, (1,), (3,))
    par = params_a(2, 2)
    start_sums(3, layer_down(functools.partial(norm_a, 3, 0, par, up=False)))
    start_cols(4)

    wait_row_sends(3, (0,))
    wait_col_sends(3, (0,), (0,))
    wait_cols(4)
    par = params_b(3, gd)
    start_sums(4, layer_b(0, functools.partial(norm_b, 4, 0, par), True))
    start_cols(5)

    wait_row_sends(4)
    wait_col_sends(4)
    wait_cols(5)
    par = params_b(4, gb.at[0])
    start_sums(5, layer_b(1, functools.partial(norm_b, 5, 1, par), False))

    wait_row_sends(5)
    wait_col_sends(5)
    par = params_b(5, gb.at[1])
    halves = [tuple(p[h:h + 1] for p in par) for h in range(2)]

    def finish(i, carry):
        for r in range(low_h):
            vals = [bn(zb[0, i, pl.ds((r * 2 + h) * half_w, half_w), :], halves[h]) for h in range(2)]
            yo[i, r] = jnp.concatenate(vals, axis=1).astype(BF16)
        pltpu.make_async_copy(yo.at[i], y.at[i], out_sem.at[i]).start()
        return carry

    lax.fori_loop(0, n_img, finish, 0)

    for e in range(6):
        buf = sums_refs(e)
        rest = buf.at[pl.ds(0, n_dev - 1)]
        pltpu.make_async_copy(rest, rest, st_send.at[e]).wait()

    def drain(i, carry):
        pltpu.make_async_copy(yo.at[i], y.at[i], out_sem.at[i]).wait()
        return carry

    lax.fori_loop(0, n_img, drain, 0)


def net(rows_n, cols_n, x, w_a, bn_a, w_down, bn_down, w_b, bn_b):
    n_img, height, width, chan = x.shape
    half_w, low_h = width // 2, height // 2
    n_dev = rows_n * cols_n
    fstride = half_w + 2 * PAD
    vmem, dma = pltpu.VMEM, pltpu.SemaphoreType.DMA
    scratch = [
        vmem((n_img, height, width, chan), BF16),
        vmem((2, n_img, width, chan), BF16),
        vmem(((height + 2) * (width + 2 * PAD), chan), F32),
        vmem((2, n_img, height * 2 * half_w, chan), F32),
        vmem((2, n_img, low_h * 2 * half_w, chan), F32),
        vmem((3, 2, n_img, 2 * half_w, chan), F32),
        vmem((2, 2, n_img, 2 * half_w, chan), F32),
        vmem(((height + 2) * 2 * fstride, chan), F32),
        vmem(((low_h + 2) * 2 * fstride, chan), F32),
        vmem((height + 2, half_w, 2 * chan), BF16),
        vmem((height + 2, half_w, 2 * chan), BF16),
        vmem((3, low_h + 2, half_w, 2 * chan), BF16),
        vmem((6, 2, n_img, height, chan), F32),
        vmem((6, 2, n_img, height, chan), F32),
        vmem((4, 4, n_img, 1, chan), F32),
        vmem((4, 4, n_img, 1, chan), F32),
        vmem((2, 4, n_img, 2, chan), F32),
        vmem((2, 4, n_img, 2, chan), F32),
        vmem((3, n_dev, 2, chan), F32),
        vmem((3, n_dev, 4, chan), F32),
        vmem((3, 3, 2 * chan, 2 * chan), BF16),
        vmem((3, 3, 2 * chan, 2 * chan), BF16),
        vmem((3, 2, 2 * chan, 2 * chan), BF16),
        vmem(w_b.shape, BF16),
        vmem(bn_a.shape, F32),
        vmem(bn_down.shape, F32),
        vmem(bn_b.shape, F32),
        vmem((n_img, low_h, half_w, 2 * chan), BF16),
        dma((n_img,)),
        dma((13,)),
        dma((6, 2, n_img)),
        dma((6, 2, n_img)),
        dma((6, 2)),
        dma((6, 2)),
        dma((6, 4)),
        dma((6, 4)),
        dma((6,)),
        dma((6,)),
        dma((n_img,)),
    ]
    any_spec = pl.BlockSpec(memory_space=pl.ANY)
    return pl.pallas_call(
        functools.partial(net_kernel, (rows_n, cols_n, n_img, height, width, chan)),
        out_shape=jax.ShapeDtypeStruct((n_img, low_h, half_w, 2 * chan), BF16),
        in_specs=[any_spec] * 7,
        out_specs=any_spec,
        scratch_shapes=scratch,
        compiler_params=pltpu.CompilerParams(collective_id=0, has_side_effects=True, vmem_limit_bytes=56 * 1024 * 1024),
        name="conv_bn_net",
    )(x, w_a, bn_a, w_down, bn_down, w_b, bn_b)


def solution(mesh):
    tile_spec = P("dp", "sp", "sp2", None)
    per_device = functools.partial(net, mesh.shape["sp"], mesh.shape["sp2"])
    return jax.shard_map(per_device, mesh=mesh, in_specs=(tile_spec, P(), P(), P(), P(), P(), P()), out_specs=tile_spec, check_vma=False)
```

time: 411 us -> 85.7 us (0.21)
  blocking collectives: 269 us -> 0 us
  Pallas kernels: 0 us -> 83.3 us
  waiting for transfers between devices: 50.9 us -> 0 us
  starting transfers between devices: 47.4 us -> 0 us
  matrix products: 26.9 us -> 0 us
  other arithmetic: 10.5 us -> 0 us
    psum x6 -> x0, blocking collectives: 269 us -> none  [conv_bn(): moments = lax.psum(moments, ('sp2', 'sp'))]
    pallas_call x0 -> x1, Pallas kernels: none -> 83.3 us  [net(): pl.pallas_call(functools.partial(net_kernel, (rows_n, cols_n, n_img, heig...]
    ppermute x22 -> x0, waiting for transfers between devices: 50.9 us -> none  [the longest x12 45.2 us: edge_extend(): lax.ppermute(first_line, axis_name, perm=[(device + 1, device) for device...]
    ppermute x22 -> x0, starting transfers between devices: 47.4 us -> none  [the longest x10 26 us: edge_extend(): lax.ppermute(last_line, axis_name, perm=[(device, device + 1) for device...]
    conv_general_dilated x6 -> x0, matrix products: 26.9 us -> none  [conv_bn(): lax.conv_general_dilated(extended, weight, (stride, stride), 'VALID', dim...]
    convert_element_type x6 -> x0, other arithmetic: 10.4 us -> none  [conv_bn(): return jnp.maximum(normed, 0.0).astype(jnp.bfloat16)]
  transfers between devices with their start and end apart: 22 -> 0, of which waited for: 17 -> 0; matrix products, arithmetic and copies ran while one was open for 0% -> 0% of each run, Pallas kernels for 0% -> 0%
where the time goes in v1:
time: 85.7 us; the launch traced here: 85.6 us
  Pallas kernels  83.3 us (97%)
  local copies, waits for them, and re-layouts  2.3 us (3%)
    pallas_call x1, Pallas kernels, net(): pl.pallas_call(functools.partial(net_kernel, (rows_n, cols_n, n_img, heig...  83.3 us
    unnamed x1, local copies, waits for them, and re-layouts  2.3 us

profile of v1, /device:TPU:97, one launch (start us, length us, event | category | flops | bytes accessed | tf_op | source)
XLA Modules:
  0.0 85.6 jit_solution(10216836871868215077)
XLA Ops:
  0.0 83.3 %conv_bn_net.1 = bf16[8,4,64,256]{3,2,1,0:T(8,128)(2,1)} custom-call(bf16[8,8,128,128]{3,2,1,0:T(8,128)(2,1)} %x.1, bf16[3,3,3,128,128]{4,3,2,1,0:T(8,128)(2,1)} %w_a.1, f32[3,2,128]{2,1,0:T(2,128)} %bn_a.1, bf16[3,3,128,256]{3,2,1,0:T(8,128)(2,1)} %w_down.1, f32[2,256]{1,0:T(2,128)} %bn_down.1, bf16[2,3,3,256,256]{4,3,2,1,0:T(8,128)(2,1)} %w_b.1, ...), custom_call_target="tpu_custom_call" | custom-call | tf_op jit(solution)/shard_map/conv_bn_net/pallas_call | solution.py:501
  83.3 2.3 %copy.9 = bf16[8,4,64,256]{3,2,1,0:T(8,128)(2,1)} copy(bf16[8,4,64,256]{3,2,1,0:T(8,128)(2,1)} %conv_bn_net.1) | data formatting | bytes 2097152

commit v2 on v1

v2 whole, which is shorter than its diff:
```python
import functools

import jax
import jax.numpy as jnp
from jax import lax
from jax.experimental import pallas as pl
from jax.experimental.pallas import tpu as pltpu
from jax.sharding import PartitionSpec as P

MESH = pl.DeviceIdType.MESH
F32 = jnp.float32
BF16 = jnp.bfloat16
EPS = 1e-5
PAD = 8
SIDES = (0, 1)
CORNERS = (0, 1, 2, 3)
TAPS = range(3)
EARLY_A = 4
EARLY_B = 2


def net_kernel(dims, x, w_a, bn_a, w_down, bn_down, w_b, bn_b, zo, so,
               xin, xh, xf0, xf1, za0, za1, zb0, zb1, ha, hb, yfa0, yfa1, yfb0, yfb1, ya0, ya1, sa0, sa1, yb0, yb1,
               cs, cl, ksa, kla, ksb, klb, ta, tb, wy, ws, wd, wb, ga, gd, gb,
               in_sem, w_sem, row_recv, row_send, col_recv, col_send, cor_recv, cor_send, st_recv, st_send):
    rows_n, cols_n, n_img, height, width, chan = dims
    n_dev = rows_n * cols_n
    half_w, low_h = width // 2, height // 2
    line, wide = 2 * half_w, 2 * chan
    xstride = width + 2 * PAD
    fstride = half_w + 2 * PAD
    xfs, zas, zbs, yfas, yfbs, yas, sas, ybs = (xf0, xf1), (za0, za1), (zb0, zb1), (yfa0, yfa1), (yfb0, yfb1), (ya0, ya1), (sa0, sa1), (yb0, yb1)
    sp = lax.axis_index("sp")
    sp2 = lax.axis_index("sp2")
    me = sp2 * rows_n + sp
    has_up = sp > 0
    has_down = sp < rows_n - 1
    has_left = sp2 > 0
    has_right = sp2 < cols_n - 1
    row_ok = (has_up, has_down)
    col_ok = (has_left, has_right)
    cor_ok = tuple(r & c for r in row_ok for c in col_ok)

    def device(d_sp, d_sp2):
        return {"sp": sp + d_sp, "sp2": sp2 + d_sp2}

    for i in range(n_img):
        pltpu.make_async_copy(x.at[i], xin.at[i], in_sem.at[i]).start()
    weight_copies = []
    for kx, dst, k0, n0 in ((1, wy, 0, 0), (1, wy, chan, chan), (0, wy, 0, chan), (2, wy, chan, 0), (0, ws, 0, 0), (2, ws, chan, chan)):
        weight_copies.append((w_a.at[:, :, kx], dst.at[:, :, pl.ds(k0, chan), pl.ds(n0, chan)]))
    weight_copies.append((w_down.at[:, 0], wd.at[:, 0, pl.ds(0, chan), :]))
    weight_copies.append((w_down.at[:, 1], wd.at[:, 0, pl.ds(chan, chan), :]))
    weight_copies.append((w_down.at[:, 2], wd.at[:, 1, pl.ds(chan, chan), :]))
    weight_copies.append((w_b, wb))
    weight_copies.append((bn_a, ga))
    weight_copies.append((bn_down, gd))
    weight_copies.append((bn_b, gb))
    weight_copies = [pltpu.make_async_copy(s, d, w_sem.at[k]) for k, (s, d) in enumerate(weight_copies)]
    for copy in weight_copies:
        copy.start()

    barrier = pltpu.get_barrier_semaphore()

    chips = rows_n // 2
    chip, core = lax.div(sp, 2), lax.rem(sp, 2)
    lines = [[lax.rem(chip + d, chips) * 2 + c for c in (core, 1 - core)] for d in range(chips)]
    files = [lax.rem(sp2 + d, cols_n) for d in range(cols_n)]
    hops = {(dx, dy): min(dx, chips - dx) + min(dy, cols_n - dy) for dx in range(chips) for dy in range(cols_n)}
    others = [{"sp": lines[dx][flip], "sp2": files[dy]} for dx, dy in sorted(hops, key=lambda o: -hops[o]) for flip in (1, 0) if (dx, dy, flip) != (0, 0, 0)]

    for other in others:
        pl.semaphore_signal(barrier, inc=1, device_id=other, device_id_type=MESH)

    zeros = jnp.zeros((chan, chan), BF16)
    for layer in TAPS:
        for ky in TAPS:
            ws[layer, ky, 0:chan, chan:wide] = zeros
            ws[layer, ky, chan:wide, 0:chan] = zeros
    for ky in TAPS:
        wd[ky, 1, 0:chan, :] = jnp.zeros((chan, wide), BF16)

    for i in range(n_img):
        pltpu.make_async_copy(x.at[i], xin.at[i], in_sem.at[i]).wait()
    for i in range(n_img):
        for side, col0, pick in ((0, 0, 0), (1, width - 16, 15)):
            blk = xin[i, :, col0:col0 + 16, :].astype(F32)
            yfa0[0:height * 16, :] = blk.reshape(height * 16, chan)
            edge = yfa0[pl.ds(pick, height, stride=16), :]
            cs[0, side, i] = edge
            ksa[0, side, i] = edge[0:1]
            ksa[0, 2 + side, i] = edge[height - 1:height]

    pl.semaphore_wait(barrier, n_dev - 1)

    def cor_bufs(e):
        return (ksa.at[e], kla.at[e]) if e < 4 else (ksb.at[e - 4], klb.at[e - 4])

    def start_cols(e, sides=SIDES, corners=CORNERS):
        for side in sides:
            d = -1 if side == 0 else 1

            @pl.when(col_ok[side])
            def _():
                pltpu.make_async_remote_copy(cs.at[e, side], cl.at[e, 1 - side], col_send.at[e, side], col_recv.at[e, 1 - side],
                                             device_id=device(0, d), device_id_type=MESH).start()
        src, dst = cor_bufs(e)
        for corner in corners:
            d_sp = -1 if corner < 2 else 1
            d_sp2 = -1 if corner % 2 == 0 else 1

            @pl.when(cor_ok[corner])
            def _():
                pltpu.make_async_remote_copy(src.at[corner], dst.at[3 - corner], cor_send.at[e, corner], cor_recv.at[e, 3 - corner],
                                             device_id=device(d_sp, d_sp2), device_id_type=MESH).start()

    def wait_cols(e, sides=SIDES, corners=CORNERS):
        for side in sides:
            @pl.when(col_ok[side])
            def _():
                pltpu.make_async_copy(cl.at[e, side], cl.at[e, side], col_recv.at[e, side]).wait()
        src, dst = cor_bufs(e)
        for corner in corners:
            @pl.when(cor_ok[corner])
            def _():
                pltpu.make_async_copy(dst.at[corner], dst.at[corner], cor_recv.at[e, corner]).wait()

    def wait_col_sends(e, sides=SIDES, corners=CORNERS):
        for side in sides:
            @pl.when(col_ok[side])
            def _():
                pltpu.make_async_copy(cs.at[e, side], cs.at[e, side], col_send.at[e, side]).wait()
        src, dst = cor_bufs(e)
        for corner in corners:
            @pl.when(cor_ok[corner])
            def _():
                pltpu.make_async_copy(src.at[corner], src.at[corner], cor_send.at[e, corner]).wait()

    def row_landing(e, side):
        if e == 0:
            return xh.at[side]
        return ha.at[e - 1, side] if e < 4 else hb.at[e - 4, side]

    def row_source(e, side, i):
        if e == 0:
            return xin.at[i, 0 if side == 0 else height - 1]
        src, n_rows = (zas[(e - 1) % 2], height) if e < 4 else (zbs[e % 2], low_h)
        return src.at[i, pl.ds(0 if side == 0 else (n_rows - 1) * line, line)]

    def send_rows(e, sides, images, cond=True):
        for side in sides:
            @pl.when(row_ok[side] & cond)
            def _():
                for i in images:
                    pltpu.make_async_remote_copy(row_source(e, side, i), row_landing(e, 1 - side).at[i], row_send.at[e, side, i],
                                                 row_recv.at[e, 1 - side, i], device_id=device(-1 if side == 0 else 1, 0),
                                                 device_id_type=MESH).start()

    def wait_rows(e, sides, images, cond=True):
        for side in sides:
            @pl.when(row_ok[side] & cond)
            def _():
                for i in images:
                    ref = row_landing(e, side).at[i]
                    pltpu.make_async_copy(ref, ref, row_recv.at[e, side, i]).wait()

    def wait_row_sends(e, sides=SIDES):
        for side in sides:
            @pl.when(row_ok[side])
            def _():
                ref = row_landing(e, side)

                def one(i, carry):
                    pltpu.make_async_copy(ref.at[i], ref.at[i], row_send.at[e, side, i]).wait()
                    return carry

                lax.fori_loop(0, n_img, one, 0)

    def sums_refs(e):
        return ta.at[e] if e < 3 else tb.at[e - 3]

    def start_sums(e, part):
        buf = sums_refs(e)
        buf[me] = part

        for other in others:
            pltpu.make_async_remote_copy(buf.at[me], buf.at[me], st_send.at[e], st_recv.at[e], device_id=other, device_id_type=MESH).start()

    def finish_sums(e, num_pos):
        buf = sums_refs(e)
        rest = buf.at[pl.ds(0, n_dev - 1)]
        pltpu.make_async_copy(rest, rest, st_recv.at[e]).wait()
        total = jnp.sum(buf[...], axis=0) / num_pos
        lines = total.shape[0] // 2
        mean = total[0:lines]
        var = total[lines:] - mean * mean
        return mean, lax.rsqrt(var + EPS)

    def bn(z, par):
        mean, inv, gain, shift = par
        return jnp.maximum(gain * (z - mean) * inv + shift, 0.0)

    def keep(cond, val):
        return jnp.where(cond, val, 0.0)

    def prep_x(i, k):
        xf, ya, sa = xfs[k], yas[k], sas[k]
        last = height + 1
        for r in range(height):
            xf[pl.ds((r + 1) * xstride + PAD, width), :] = xin[i, r].astype(F32)
        xf[pl.ds(PAD, width), :] = keep(has_up, xh[0, i].astype(F32))
        xf[pl.ds(last * xstride + PAD, width), :] = keep(has_down, xh[1, i].astype(F32))
        xf[pl.ds(xstride + PAD - 1, height, stride=xstride), :] = keep(has_left, cl[0, 0, i])
        xf[pl.ds(xstride + PAD + width, height, stride=xstride), :] = keep(has_right, cl[0, 1, i])
        for corner in CORNERS:
            row = 0 if corner < 2 else last
            col = PAD - 1 if corner % 2 == 0 else PAD + width
            xf[row * xstride + col:row * xstride + col + 1, :] = keep(cor_ok[corner], kla[0, corner, i])
        for r in range(height + 2):
            base = r * xstride + PAD
            even = xf[pl.ds(base, half_w, stride=2), :]
            odd = xf[pl.ds(base + 1, half_w, stride=2), :]
            before = xf[pl.ds(base - 1, half_w, stride=2), :]
            after = xf[pl.ds(base + 2, half_w, stride=2), :]
            ya[r] = jnp.concatenate([even, odd], axis=1).astype(BF16)
            sa[r] = jnp.concatenate([before, after], axis=1).astype(BF16)

    def norm_a(e, par, i, k, up=True):
        za, yfa, ya, sa = zas[(e - 1) % 2], yfas[k], yas[k], sas[k]
        last = height + 1
        lo = 0 if up else 1
        for r in range(lo, height + 2):
            if r == 0:
                val = keep(has_up, bn(ha[e - 1, 0, i], par))
            elif r == last:
                val = keep(has_down, bn(ha[e - 1, 1, i], par))
            else:
                val = bn(za[i, pl.ds((r - 1) * line, line), :], par)
            base = r * 2 * fstride + PAD
            yfa[base:base + half_w, :] = val[0:half_w]
            yfa[base + fstride:base + fstride + half_w, :] = val[half_w:]
        if up:
            yfa[pl.ds(3 * fstride + PAD - 1, height, stride=2 * fstride), :] = keep(has_left, bn(cl[e, 0, i], par))
        yfa[pl.ds(2 * fstride + PAD + half_w, height, stride=2 * fstride), :] = keep(has_right, bn(cl[e, 1, i], par))
        for corner in CORNERS if up else (3,):
            row = 0 if corner < 2 else last
            at = row * 2 * fstride + (fstride + PAD - 1 if corner % 2 == 0 else PAD + half_w)
            yfa[at:at + 1, :] = keep(cor_ok[corner], bn(kla[e, corner, i], par))
        for r in range(lo, height + 2):
            base = r * 2 * fstride + PAD
            even = yfa[base:base + half_w, :]
            odd = yfa[base + fstride:base + fstride + half_w, :]
            before = yfa[base + fstride - 1:base + fstride - 1 + half_w, :]
            after = yfa[base + 1:base + 1 + half_w, :]
            ya[r] = jnp.concatenate([even, odd], axis=1).astype(BF16)
            sa[r] = jnp.concatenate([before, after], axis=1).astype(BF16)

    def norm_b(e, par, i, k):
        zb, yfb, yb = zbs[e % 2], yfbs[k], ybs[k]
        last = low_h + 1
        halves = [tuple(p[h:h + 1] for p in par) for h in SIDES]
        tall = tuple(jnp.concatenate([p] * low_h, axis=0) for p in par)
        for r in range(low_h + 2):
            for h in SIDES:
                if r == 0:
                    val = keep(has_up, bn(hb[e - 4, 0, i, pl.ds(h * half_w, half_w), :], halves[h]))
                elif r == last:
                    val = keep(has_down, bn(hb[e - 4, 1, i, pl.ds(h * half_w, half_w), :], halves[h]))
                else:
                    val = bn(zb[i, pl.ds(((r - 1) * 2 + h) * half_w, half_w), :], halves[h])
                base = (r * 2 + h) * fstride + PAD
                yfb[base:base + half_w, :] = val
        yfb[pl.ds(2 * fstride + PAD - 1, 2 * low_h, stride=fstride), :] = keep(has_left, bn(cl[e, 0, i], tall))
        yfb[pl.ds(2 * fstride + PAD + half_w, 2 * low_h, stride=fstride), :] = keep(has_right, bn(cl[e, 1, i], tall))
        for corner in CORNERS:
            row = 0 if corner < 2 else last
            val = keep(cor_ok[corner], bn(klb[e - 4, corner, i], par))
            for h in SIDES:
                at = (row * 2 + h) * fstride + (PAD - 1 if corner % 2 == 0 else PAD + half_w)
                yfb[at:at + 1, :] = val[h:h + 1]
        for r in range(low_h + 2):
            base = r * 2 * fstride + PAD
            for kx in TAPS:
                at = base + kx - 1
                yb[kx, r] = jnp.concatenate([yfb[at:at + half_w, :], yfb[at + fstride:at + fstride + half_w, :]], axis=1).astype(BF16)

    def add_sums(acc, carry):
        tiles = acc.reshape(acc.shape[0] // 8, 8, acc.shape[1])
        return carry[0] + jnp.sum(tiles, axis=0), carry[1] + jnp.sum(tiles * tiles, axis=0)

    zero_sums = (jnp.zeros((8, wide), F32), jnp.zeros((8, wide), F32))

    def edges_a(e, i):
        za = zas[(e - 1) % 2]
        first = za[i, pl.ds(0, height, stride=line), :]
        final = za[i, pl.ds(line - 1, height, stride=line), :]
        for side, edge in enumerate((first, final)):
            cs[e, side, i] = edge
            ksa[e, side, i] = edge[0:1]
            ksa[e, 2 + side, i] = edge[height - 1:height]

    def edges_b(e, i):
        zb = zbs[e % 2]
        first = zb[i, pl.ds(0, 2 * low_h, stride=half_w), :]
        final = zb[i, pl.ds(half_w - 1, 2 * low_h, stride=half_w), :]
        for side, edge in enumerate((first, final)):
            cs[e, side, i] = edge
            ksb[e - 4, side, i] = edge[0:2]
            ksb[e - 4, 2 + side, i] = edge[2 * low_h - 2:2 * low_h]

    def store_z(ref, i, acc, rows):
        for r in range(rows):
            at = r * line
            ref[i, at:at + half_w, :] = acc[r * half_w:(r + 1) * half_w, 0:chan]
            ref[i, at + half_w:at + line, :] = acc[r * half_w:(r + 1) * half_w, chan:wide]

    def products(pairs):
        acc = None
        for lhs, w in pairs:
            d = jnp.dot(lhs, w, preferred_element_type=F32)
            acc = d if acc is None else acc + d
        return acc

    def conv_a(layer, i, k, carry):
        pairs = []
        for ky in TAPS:
            for ref, w in ((yas[k], wy), (sas[k], ws)):
                pairs.append((ref[ky:ky + height].reshape(height * half_w, wide), w[layer, ky]))
        acc = products(pairs)
        store_z(zas[layer % 2], i, acc, height)
        edges_a(layer + 1, i)
        return add_sums(acc, carry)

    def conv_down(i, k, carry):
        pairs = []
        for ky in TAPS:
            for part, ref in enumerate((yas[k], sas[k])):
                pairs.append((jnp.concatenate([ref[1 + 2 * r + ky] for r in range(low_h)], axis=0), wd[ky, part]))
        acc = products(pairs)
        store_z(zbs[0], i, acc, low_h)
        edges_b(4, i)
        return add_sums(acc, carry)

    def conv_b(layer, i, k, carry):
        pairs = []
        for ky in TAPS:
            for kx in TAPS:
                pairs.append((ybs[k][kx, ky:ky + low_h].reshape(low_h * half_w, wide), wb[layer, ky, kx]))
        acc = products(pairs)
        if layer == 0:
            store_z(zb1, i, acc, low_h)
            edges_b(5, i)
        else:
            zo[i] = acc.reshape(low_h, half_w, wide)
        return add_sums(acc, carry)

    def layer(e, prep, conv, in_sides, out_sides, early):
        wait_rows(e, in_sides, (0,))
        prep(0, 0)

        def pair(j, carry):
            i = 2 * j
            wait_rows(e, in_sides, (i + 1,))
            wait_rows(e, in_sides, (i + 2,), i + 2 < n_img)
            prep(i + 1, 1)
            carry = conv(i, 0, carry)
            prep(lax.min(i + 2, n_img - 1), 0)
            carry = conv(i + 1, 1, carry)
            send_rows(e + 1, out_sides, (i, i + 1), i < early)
            return carry

        s1, s2 = lax.fori_loop(0, n_img // 2, pair, zero_sums)
        s1, s2 = (jnp.sum(s, axis=0, keepdims=True) for s in (s1, s2))
        if e < 3:
            part = [s1[:, 0:chan] + s1[:, chan:], s2[:, 0:chan] + s2[:, chan:]]
        else:
            part = [s1[:, 0:chan], s1[:, chan:], s2[:, 0:chan], s2[:, chan:]]
        start_sums(e, jnp.concatenate(part, axis=0))
        if e < 5:
            both = len(out_sides) == 2
            start_cols(e + 1, SIDES if both else (0,), CORNERS if both else (0,))
            send_rows(e + 1, out_sides, range(early, n_img))

    send_rows(0, SIDES, range(n_img))
    start_cols(0)
    for copy in weight_copies:
        copy.wait()
    wait_cols(0)

    pos_a = n_dev * n_img * height * width
    pos_b = n_dev * n_img * low_h * half_w

    def params_a(e, layer):
        mean, inv = finish_sums(e, pos_a)
        return mean, inv, ga[layer, 0:1], ga[layer, 1:2]

    def params_b(e, ref):
        mean, inv = finish_sums(e, pos_b)
        gain = jnp.concatenate([ref[0:1, 0:chan], ref[0:1, chan:]], axis=0)
        shift = jnp.concatenate([ref[1:2, 0:chan], ref[1:2, chan:]], axis=0)
        return mean, inv, gain, shift

    part = functools.partial
    layer(0, prep_x, part(conv_a, 0), SIDES, SIDES, EARLY_A)

    wait_row_sends(0)
    wait_col_sends(0)
    wait_cols(1)
    layer(1, part(norm_a, 1, params_a(0, 0)), part(conv_a, 1), SIDES, SIDES, EARLY_A)

    wait_row_sends(1)
    wait_col_sends(1)
    wait_cols(2)
    layer(2, part(norm_a, 2, params_a(1, 1)), part(conv_a, 2), SIDES, (0,), EARLY_A)

    wait_row_sends(2)
    wait_col_sends(2)
    wait_cols(3, (1,), (3,))
    layer(3, part(norm_a, 3, params_a(2, 2), up=False), conv_down, (1,), SIDES, EARLY_B)

    wait_row_sends(3, (0,))
    wait_col_sends(3, (0,), (0,))
    wait_cols(4)
    layer(4, part(norm_b, 4, params_b(3, gd)), part(conv_b, 0), SIDES, SIDES, EARLY_B)

    wait_row_sends(4)
    wait_col_sends(4)
    wait_cols(5)
    layer(5, part(norm_b, 5, params_b(4, gb.at[0])), part(conv_b, 1), SIDES, (), 0)

    wait_row_sends(5)
    wait_col_sends(5)
    mean, inv = finish_sums(5, pos_b)
    so[...] = jnp.concatenate([mean, inv], axis=0)

    for e in range(6):
        buf = sums_refs(e)
        rest = buf.at[pl.ds(0, n_dev - 1)]
        pltpu.make_async_copy(rest, rest, st_send.at[e]).wait()


def net(rows_n, cols_n, x, w_a, bn_a, w_down, bn_down, w_b, bn_b):
    n_img, height, width, chan = x.shape
    half_w, low_h = width // 2, height // 2
    n_dev = rows_n * cols_n
    vmem, dma = pltpu.VMEM, pltpu.SemaphoreType.DMA
    line, wide = 2 * half_w, 2 * chan
    plane = half_w + 2 * PAD
    a_sums, b_sums = 3, 3
    n_ex = a_sums + b_sums
    two, corners = len(SIDES), len(CORNERS)
    scratch = [
        vmem(x.shape, BF16),
        vmem((two, n_img, width, chan), BF16),
        *[vmem(((height + 2) * (width + 2 * PAD), chan), F32)] * two,
        *[vmem((n_img, height * line, chan), F32)] * two,
        *[vmem((n_img, low_h * line, chan), F32)] * two,
        vmem((a_sums, two, n_img, line, chan), F32),
        vmem((b_sums - 1, two, n_img, line, chan), F32),
        *[vmem(((height + 2) * 2 * plane, chan), F32)] * two,
        *[vmem(((low_h + 2) * 2 * plane, chan), F32)] * two,
        *[vmem((height + 2, half_w, wide), BF16)] * 4,
        *[vmem((3, low_h + 2, half_w, wide), BF16)] * two,
        *[vmem((n_ex, two, n_img, height, chan), F32)] * two,
        *[vmem((a_sums + 1, corners, n_img, 1, chan), F32)] * two,
        *[vmem((b_sums - 1, corners, n_img, 2, chan), F32)] * two,
        vmem((a_sums, n_dev, 2, chan), F32),
        vmem((b_sums, n_dev, 4, chan), F32),
        *[vmem((a_sums, 3, wide, wide), BF16)] * two,
        vmem((3, two, wide, wide), BF16),
        vmem(w_b.shape, BF16),
        vmem(bn_a.shape, F32),
        vmem(bn_down.shape, F32),
        vmem(bn_b.shape, F32),
        dma((n_img,)),
        dma((13,)),
        *[dma((n_ex, two, n_img))] * two,
        *[dma((n_ex, two))] * two,
        *[dma((n_ex, corners))] * two,
        *[dma((n_ex,))] * two,
    ]
    hbm_spec = pl.BlockSpec(memory_space=pltpu.HBM)
    z, stats = pl.pallas_call(
        functools.partial(net_kernel, (rows_n, cols_n, n_img, height, width, chan)),
        out_shape=(jax.ShapeDtypeStruct((n_img, low_h, half_w, wide), F32), jax.ShapeDtypeStruct((4, chan), F32)),
        in_specs=[hbm_spec] * 7,
        out_specs=(pl.BlockSpec(memory_space=pltpu.VMEM),) * 2,
        scratch_shapes=scratch,
        compiler_params=pltpu.CompilerParams(collective_id=0, has_side_effects=True, vmem_limit_bytes=40 * 1024 * 1024),
        name="conv_bn_net",
    )(x, w_a, bn_a, w_down, bn_down, w_b, bn_b)
    mean, inv = stats.reshape(2, wide)
    gain, shift = bn_b[1]
    return jnp.maximum(gain * (z - mean) * inv + shift, 0.0).astype(BF16)


def solution(mesh):
    tile_spec = P("dp", "sp", "sp2", None)
    per_device = functools.partial(net, mesh.shape["sp"], mesh.shape["sp2"])
    return jax.shard_map(per_device, mesh=mesh, in_specs=(tile_spec, P(), P(), P(), P(), P(), P()), out_specs=tile_spec, check_vma=False)
```

time: 85.7 us -> 80.1 us (0.935)
  Pallas kernels: 83.3 us -> 70.1 us
  local copies, waits for them, and re-layouts: 2.3 us -> 8.3 us
  other arithmetic: 0 us -> 1.39 us
    pallas_call x1, Pallas kernels: 83.3 us -> 70.1 us  [net(): pl.pallas_call(functools.partial(net_kernel, (rows_n, cols_n, n_img, heig...]
    unnamed x1 -> x14, local copies, waits for them, and re-layouts: 2.3 us -> 7.54 us
    convert_element_type x0 -> x1, other arithmetic: none -> 1.39 us  [net(): return jnp.maximum(gain * (z - mean) * inv + shift, 0.0).astype(BF16)]
where the time goes in v2:
time: 80.1 us; the launch traced here: 79.8 us
  Pallas kernels  70.1 us (88%)
  local copies, waits for them, and re-layouts  8.3 us (10%)
  other arithmetic  1.39 us (2%)
    pallas_call x1, Pallas kernels, net(): pl.pallas_call(functools.partial(net_kernel, (rows_n, cols_n, n_img, heig...  70.1 us
    unnamed x14, local copies, waits for them, and re-layouts  7.54 us

profile of v2, /device:TPU:97, one launch (start us, length us, event | category | flops | bytes accessed | tf_op | source)
XLA Modules:
  0.0 79.8 jit_solution(10606579095077878459)
XLA Ops:
  0.0 0.8 fusion
  0.8 0.0 copy-start
  0.8 1.7 %copy-done = bf16[2,3,3,256,256]{4,3,2,1,0:T(8,128)(2,1)S(1)} copy-done((bf16[2,3,3,256,256]{4,3,2,1,0:T(8,128)(2,1)S(1)}, bf16[2,3,3,256,256]{4,3,2,1,0:T(8,128)(2,1)}, u32[]{:S(2)}) %copy-start) | copy-done | bytes 2359320
  2.4 0.0 copy-start.1
  2.4 1.6 %copy-done.1 = bf16[8,8,128,128]{3,2,1,0:T(8,128)(2,1)S(1)} copy-done((bf16[8,8,128,128]{3,2,1,0:T(8,128)(2,1)S(1)}, bf16[8,8,128,128]{3,2,1,0:T(8,128)(2,1)}, u32[]{:S(2)}) %copy-start.1) | copy-done | bytes 2097176
  4.0 0.0 copy-start.2
  4.0 1.2 %copy-done.2 = bf16[3,3,3,128,128]{4,3,2,1,0:T(8,128)(2,1)S(1)} copy-done((bf16[3,3,3,128,128]{4,3,2,1,0:T(8,128)(2,1)S(1)}, bf16[3,3,3,128,128]{4,3,2,1,0:T(8,128)(2,1)}, u32[]{:S(2)}) %copy-start.2) | copy-done | bytes 884760
  5.2 0.0 copy-start.3
  5.2 1.1 %copy-done.3 = bf16[3,3,128,256]{3,2,1,0:T(8,128)(2,1)S(1)} copy-done((bf16[3,3,128,256]{3,2,1,0:T(8,128)(2,1)S(1)}, bf16[3,3,128,256]{3,2,1,0:T(8,128)(2,1)}, u32[]{:S(2)}) %copy-start.3) | copy-done | bytes 589848
  6.3 0.0 copy-start.4
  6.3 0.7 copy-done.4
  6.9 0.0 copy-start.5
  6.9 0.7 copy-done.5
  7.6 0.0 copy-start.6
  7.6 0.7 copy-done.6
  8.3 70.1 %conv_bn_net.1 = (f32[8,4,64,256]{3,2,1,0:T(8,128)S(1)}, f32[4,128]{1,0:T(4,128)S(1)}) custom-call(bf16[8,8,128,128]{3,2,1,0:T(8,128)(2,1)S(1)} %copy-done.1, bf16[3,3,3,128,128]{4,3,2,1,0:T(8,128)(2,1)S(1)} %copy-done.2, f32[3,2,128]{2,1,0:T(2,128)S(1)} %copy-done.5, bf16[3,3,128,256]{3,2,1,0:T(8,128)(2,1)S(1)} %copy-done.3, f32[2,256]{1,0:T(2,128)S(1)} %copy-done.6, ...), custom_call_target="tpu_custom_call" | custom-call | tf_op jit(solution)/shard_map/conv_bn_net/pallas_call | solution.py:483
  78.4 1.4 %maximum_convert_fusion = bf16[8,4,64,256]{3,2,1,0:T(8,128)(2,1)} fusion(f32[8,4,64,256]{3,2,1,0:T(8,128)S(1)} %get-tuple-element.7, f32[256]{0:T(256)S(1)} %bitcast.7, f32[256]{0:T(256)S(1)} %get-tuple-element.12, f32[256]{0:T(256)S(1)} %get-tuple-element.11, f32[256]{0:T(256)S(1)} %bitcast.6), kind=kLoop, calls=%fused_computation | loop fusion | flops 3145728 | bytes 3149824 | tf_op jit(solution)/shard_map/convert_element_type | solution.py:494
  (1 shorter events, 0.0 us)
Async XLA Ops:
  0.8 1.7 %copy-start = (bf16[2,3,3,256,256]{4,3,2,1,0:T(8,128)(2,1)S(1)}, bf16[2,3,3,256,256]{4,3,2,1,0:T(8,128)(2,1)}, u32[]{:S(2)}) copy-start(bf16[2,3,3,256,256]{4,3,2,1,0:T(8,128)(2,1)} %w_b.1) | copy-start | bytes 7077892
  2.4 1.6 %copy-start.1 = (bf16[8,8,128,128]{3,2,1,0:T(8,128)(2,1)S(1)}, bf16[8,8,128,128]{3,2,1,0:T(8,128)(2,1)}, u32[]{:S(2)}) copy-start(bf16[8,8,128,128]{3,2,1,0:T(8,128)(2,1)} %x.1) | copy-start | bytes 6291460
  4.0 1.2 %copy-start.2 = (bf16[3,3,3,128,128]{4,3,2,1,0:T(8,128)(2,1)S(1)}, bf16[3,3,3,128,128]{4,3,2,1,0:T(8,128)(2,1)}, u32[]{:S(2)}) copy-start(bf16[3,3,3,128,128]{4,3,2,1,0:T(8,128)(2,1)} %w_a.1) | copy-start | bytes 2654212
  5.2 1.1 %copy-start.3 = (bf16[3,3,128,256]{3,2,1,0:T(8,128)(2,1)S(1)}, bf16[3,3,128,256]{3,2,1,0:T(8,128)(2,1)}, u32[]{:S(2)}) copy-start(bf16[3,3,128,256]{3,2,1,0:T(8,128)(2,1)} %w_down.1) | copy-start | bytes 1769476
  6.3 0.7 copy-start.4
  6.9 0.7 copy-start.5
  7.6 0.7 copy-start.6

commit v3 on v2

--- a/solution.py
+++ b/solution.py
@@ -19,7 +19,7 @@
 EARLY_B = 2
 
 
-def net_kernel(dims, x, w_a, bn_a, w_down, bn_down, w_b, bn_b, zo, so,
+def net_kernel(dims, x, w_a, bn_a, w_down, bn_down, w_b, bn_b, zo, mean_o, inv_o, gain_o, shift_o,
                xin, xh, xf0, xf1, za0, za1, zb0, zb1, ha, hb, yfa0, yfa1, yfb0, yfb1, ya0, ya1, sa0, sa1, yb0, yb1,
                cs, cl, ksa, kla, ksb, klb, ta, tb, wy, ws, wd, wb, ga, gd, gb,
                in_sem, w_sem, row_recv, row_send, col_recv, col_send, cor_recv, cor_send, st_recv, st_send):
@@ -431,7 +431,11 @@
     wait_row_sends(5)
     wait_col_sends(5)
     mean, inv = finish_sums(5, pos_b)
-    so[...] = jnp.concatenate([mean, inv], axis=0)
+    for out, val in ((mean_o, mean), (inv_o, inv)):
+        for h in SIDES:
+            out[:, h * chan:(h + 1) * chan] = val[h:h + 1]
+    gain_o[...] = gb[1, 0:1]
+    shift_o[...] = gb[1, 1:2]
 
     for e in range(6):
         buf = sums_refs(e)
@@ -480,17 +484,17 @@
         *[dma((n_ex,))] * two,
     ]
     hbm_spec = pl.BlockSpec(memory_space=pltpu.HBM)
-    z, stats = pl.pallas_call(
+    line_out = jax.ShapeDtypeStruct((1, wide), F32)
+    z, *vectors = pl.pallas_call(
         functools.partial(net_kernel, (rows_n, cols_n, n_img, height, width, chan)),
-        out_shape=(jax.ShapeDtypeStruct((n_img, low_h, half_w, wide), F32), jax.ShapeDtypeStruct((4, chan), F32)),
+        out_shape=(jax.ShapeDtypeStruct((n_img, low_h, half_w, wide), F32),) + (line_out,) * 4,
         in_specs=[hbm_spec] * 7,
-        out_specs=(pl.BlockSpec(memory_space=pltpu.VMEM),) * 2,
+        out_specs=(pl.BlockSpec(memory_space=pltpu.VMEM),) * 5,
         scratch_shapes=scratch,
         compiler_params=pltpu.CompilerParams(collective_id=0, has_side_effects=True, vmem_limit_bytes=40 * 1024 * 1024),
         name="conv_bn_net",
-    )(x, w_a, bn_a, w_down, bn_down, w_b, bn_b)
-    mean, inv = stats.reshape(2, wide)
-    gain, shift = bn_b[1]
+    )(*[pltpu.with_memory_space_constraint(arg, pltpu.HBM) for arg in (x, w_a, bn_a, w_down, bn_down, w_b, bn_b)])
+    mean, inv, gain, shift = [v.reshape(wide) for v in vectors]
     return jnp.maximum(gain * (z - mean) * inv + shift, 0.0).astype(BF16)
 
 

time: 80.1 us -> 70.7 us (0.88)
  local copies, waits for them, and re-layouts: 8.3 us -> 0 us
    unnamed x14 -> x0, local copies, waits for them, and re-layouts: 7.54 us -> none
    pallas_call x1, Pallas kernels: 70.1 us -> 69.3 us  [net(): pl.pallas_call(functools.partial(net_kernel, (rows_n, cols_n, n_img, heig...]
where the time goes in v3:
time: 70.7 us; the launch traced here: 70.6 us
  Pallas kernels  69.3 us (98%)
  other arithmetic  1.37 us (2%)
    pallas_call x1, Pallas kernels, net(): pl.pallas_call(functools.partial(net_kernel, (rows_n, cols_n, n_img, heig...  69.3 us

profile of v3, /device:TPU:97, one launch (start us, length us, event | category | flops | bytes accessed | tf_op | source)
XLA Modules:
  0.0 70.6 jit_solution(1644919442517170199)
XLA Ops:
  0.0 69.3 %conv_bn_net.1 = (f32[8,4,64,256]{3,2,1,0:T(8,128)S(1)}, f32[1,256]{1,0:T(1,128)S(1)}, f32[1,256]{1,0:T(1,128)S(1)}, f32[1,256]{1,0:T(1,128)S(1)}, f32[1,256]{1,0:T(1,128)S(1)}) custom-call(bf16[8,8,128,128]{3,2,1,0:T(8,128)(2,1)} %x.1, bf16[3,3,3,128,128]{4,3,2,1,0:T(8,128)(2,1)} %w_a.1, f32[3,2,128]{2,1,0:T(2,128)} %bn_a.1, ...), custom_call_target="tpu_custom_call" | custom-call | tf_op jit(solution)/shard_map/conv_bn_net/pallas_call | solution.py:488
  69.3 1.4 %maximum_convert_fusion = bf16[8,4,64,256]{3,2,1,0:T(8,128)(2,1)} fusion(f32[8,4,64,256]{3,2,1,0:T(8,128)S(1)} %get-tuple-element.11, f32[256]{0:T(256)S(1)} %bitcast.7, f32[256]{0:T(256)S(1)} %bitcast.5, f32[256]{0:T(256)S(1)} %bitcast.4, f32[256]{0:T(256)S(1)} %bitcast.6), kind=kLoop, calls=%fused_computation | loop fusion | flops 3145728 | bytes 3149824 | tf_op jit(solution)/shard_map/convert_element_type | solution.py:498

commit v4 on v3

--- a/solution.py
+++ b/solution.py
@@ -16,13 +16,14 @@
 CORNERS = (0, 1, 2, 3)
 TAPS = range(3)
 EARLY_A = 4
-EARLY_B = 2
+EARLY_B = 4
+GROUP = 4
 
 
 def net_kernel(dims, x, w_a, bn_a, w_down, bn_down, w_b, bn_b, zo, mean_o, inv_o, gain_o, shift_o,
                xin, xh, xf0, xf1, za0, za1, zb0, zb1, ha, hb, yfa0, yfa1, yfb0, yfb1, ya0, ya1, sa0, sa1, yb0, yb1,
                cs, cl, ksa, kla, ksb, klb, ta, tb, wy, ws, wd, wb, ga, gd, gb,
-               in_sem, w_sem, row_recv, row_send, col_recv, col_send, cor_recv, cor_send, st_recv, st_send):
+               in_sem, w_sem, row_recv, row_send, col_recv, col_send, cor_recv, cor_send, st_recv, st_send, meet):
     rows_n, cols_n, n_img, height, width, chan = dims
     n_dev = rows_n * cols_n
     half_w, low_h = width // 2, height // 2
@@ -44,6 +45,38 @@
     def device(d_sp, d_sp2):
         return {"sp": sp + d_sp, "sp2": sp2 + d_sp2}
 
+    def ring(step):
+        found = []
+        for d_sp in (-step, 0, step):
+            for d_sp2 in (-step, 0, step):
+                if (d_sp or d_sp2) and abs(d_sp2) < cols_n and abs(d_sp) < rows_n:
+                    ok = (sp + d_sp >= 0) & (sp + d_sp < rows_n) & (sp2 + d_sp2 >= 0) & (sp2 + d_sp2 < cols_n)
+                    found.append((ok, device(d_sp, d_sp2)))
+        return found
+
+    def call(sem, step):
+        for ok, where in ring(step):
+            @pl.when(ok)
+            def _():
+                pl.semaphore_signal(sem, inc=1, device_id=where, device_id_type=MESH)
+
+    def hear(sem, step):
+        pl.semaphore_wait(sem, sum(ok.astype(jnp.int32) for ok, where in ring(step)))
+
+    steps = [1]
+    while 2 * steps[-1] < max(rows_n, cols_n) and len(steps) < meet.shape[0]:
+        steps.append(2 * steps[-1])
+
+    barrier = pltpu.get_barrier_semaphore()
+    call(barrier, 1)
+
+    chips = rows_n // 2
+    chip, core = lax.div(sp, 2), lax.rem(sp, 2)
+    lines = [[lax.rem(chip + d, chips) * 2 + c for c in (core, 1 - core)] for d in range(chips)]
+    files = [lax.rem(sp2 + d, cols_n) for d in range(cols_n)]
+    hops = {(dx, dy): min(dx, chips - dx) + min(dy, cols_n - dy) for dx in range(chips) for dy in range(cols_n)}
+    others = [{"sp": lines[dx][flip], "sp2": files[dy]} for dx, dy in sorted(hops, key=lambda o: -hops[o]) for flip in (1, 0) if (dx, dy, flip) != (0, 0, 0)]
+
     for i in range(n_img):
         pltpu.make_async_copy(x.at[i], xin.at[i], in_sem.at[i]).start()
     weight_copies = []
@@ -60,18 +93,6 @@
     for copy in weight_copies:
         copy.start()
 
-    barrier = pltpu.get_barrier_semaphore()
-
-    chips = rows_n // 2
-    chip, core = lax.div(sp, 2), lax.rem(sp, 2)
-    lines = [[lax.rem(chip + d, chips) * 2 + c for c in (core, 1 - core)] for d in range(chips)]
-    files = [lax.rem(sp2 + d, cols_n) for d in range(cols_n)]
-    hops = {(dx, dy): min(dx, chips - dx) + min(dy, cols_n - dy) for dx in range(chips) for dy in range(cols_n)}
-    others = [{"sp": lines[dx][flip], "sp2": files[dy]} for dx, dy in sorted(hops, key=lambda o: -hops[o]) for flip in (1, 0) if (dx, dy, flip) != (0, 0, 0)]
-
-    for other in others:
-        pl.semaphore_signal(barrier, inc=1, device_id=other, device_id_type=MESH)
-
     zeros = jnp.zeros((chan, chan), BF16)
     for layer in TAPS:
         for ky in TAPS:
@@ -85,13 +106,14 @@
     for i in range(n_img):
         for side, col0, pick in ((0, 0, 0), (1, width - 16, 15)):
             blk = xin[i, :, col0:col0 + 16, :].astype(F32)
-            yfa0[0:height * 16, :] = blk.reshape(height * 16, chan)
-            edge = yfa0[pl.ds(pick, height, stride=16), :]
+            at = side * height * 16
+            za0[i, at:at + height * 16, :] = blk.reshape(height * 16, chan)
+            edge = za0[i, pl.ds(at + pick, height, stride=16), :]
             cs[0, side, i] = edge
             ksa[0, side, i] = edge[0:1]
             ksa[0, 2 + side, i] = edge[height - 1:height]
 
-    pl.semaphore_wait(barrier, n_dev - 1)
+    hear(barrier, 1)
 
     def cor_bufs(e):
         return (ksa.at[e], kla.at[e]) if e < 4 else (ksb.at[e - 4], klb.at[e - 4])
@@ -358,18 +380,18 @@
         wait_rows(e, in_sides, (0,))
         prep(0, 0)
 
-        def pair(j, carry):
-            i = 2 * j
-            wait_rows(e, in_sides, (i + 1,))
-            wait_rows(e, in_sides, (i + 2,), i + 2 < n_img)
-            prep(i + 1, 1)
-            carry = conv(i, 0, carry)
-            prep(lax.min(i + 2, n_img - 1), 0)
-            carry = conv(i + 1, 1, carry)
-            send_rows(e + 1, out_sides, (i, i + 1), i < early)
+        def group(j, carry):
+            i = GROUP * j
+            wait_rows(e, in_sides, [i + u for u in range(1, GROUP)])
+            wait_rows(e, in_sides, (i + GROUP,), i + GROUP < n_img)
+            for u in range(GROUP):
+                nxt = u + 1
+                prep(i + nxt if nxt < GROUP else lax.min(i + nxt, n_img - 1), nxt % 2)
+                carry = conv(i + u, u % 2, carry)
+            send_rows(e + 1, out_sides, [i + u for u in range(GROUP)], i < early)
             return carry
 
-        s1, s2 = lax.fori_loop(0, n_img // 2, pair, zero_sums)
+        s1, s2 = lax.fori_loop(0, n_img // GROUP, group, zero_sums)
         s1, s2 = (jnp.sum(s, axis=0, keepdims=True) for s in (s1, s2))
         if e < 3:
             part = [s1[:, 0:chan] + s1[:, chan:], s2[:, 0:chan] + s2[:, chan:]]
@@ -381,10 +403,15 @@
             start_cols(e + 1, SIDES if both else (0,), CORNERS if both else (0,))
             send_rows(e + 1, out_sides, range(early, n_img))
 
+    call(meet.at[0], steps[0])
+    start_cols(0)
     send_rows(0, SIDES, range(n_img))
-    start_cols(0)
-    for copy in weight_copies:
+    for copy in weight_copies[:6]:
         copy.wait()
+    for k, step in enumerate(steps):
+        hear(meet.at[k], step)
+        if k + 1 < len(steps):
+            call(meet.at[k + 1], steps[k + 1])
     wait_cols(0)
 
     pos_a = n_dev * n_img * height * width
@@ -403,6 +430,8 @@
     part = functools.partial
     layer(0, prep_x, part(conv_a, 0), SIDES, SIDES, EARLY_A)
 
+    for copy in weight_copies[6:]:
+        copy.wait()
     wait_row_sends(0)
     wait_col_sends(0)
     wait_cols(1)
@@ -482,6 +511,7 @@
         *[dma((n_ex, two))] * two,
         *[dma((n_ex, corners))] * two,
         *[dma((n_ex,))] * two,
+        pltpu.SemaphoreType.REGULAR((3,)),
     ]
     hbm_spec = pl.BlockSpec(memory_space=pltpu.HBM)
     line_out = jax.ShapeDtypeStruct((1, wide), F32)

time: 70.7 us -> 72.2 us (1.021)
  Pallas kernels: 69.3 us -> 70.7 us
    pallas_call x1, Pallas kernels: 69.3 us -> 70.7 us  [net(): pl.pallas_call(functools.partial(net_kernel, (rows_n, cols_n, n_img, heig...]
where the time goes in v4:
time: 72.2 us; the launch traced here: 72.1 us
  Pallas kernels  70.7 us (98%)
  other arithmetic  1.37 us (2%)
    pallas_call x1, Pallas kernels, net(): pl.pallas_call(functools.partial(net_kernel, (rows_n, cols_n, n_img, heig...  70.7 us

profile of v4, /device:TPU:97, one launch (start us, length us, event | category | flops | bytes accessed | tf_op | source)
XLA Modules:
  0.0 72.1 jit_solution(4066555835487845041)
XLA Ops:
  0.0 70.7 %conv_bn_net.1 = (f32[8,4,64,256]{3,2,1,0:T(8,128)S(1)}, f32[1,256]{1,0:T(1,128)S(1)}, f32[1,256]{1,0:T(1,128)S(1)}, f32[1,256]{1,0:T(1,128)S(1)}, f32[1,256]{1,0:T(1,128)S(1)}) custom-call(bf16[8,8,128,128]{3,2,1,0:T(8,128)(2,1)} %x.1, bf16[3,3,3,128,128]{4,3,2,1,0:T(8,128)(2,1)} %w_a.1, f32[3,2,128]{2,1,0:T(2,128)} %bn_a.1, ...), custom_call_target="tpu_custom_call" | custom-call | tf_op jit(solution)/shard_map/conv_bn_net/pallas_call | solution.py:518
  70.7 1.4 %maximum_convert_fusion = bf16[8,4,64,256]{3,2,1,0:T(8,128)(2,1)} fusion(f32[8,4,64,256]{3,2,1,0:T(8,128)S(1)} %get-tuple-element.11, f32[256]{0:T(256)S(1)} %bitcast.7, f32[256]{0:T(256)S(1)} %bitcast.5, f32[256]{0:T(256)S(1)} %bitcast.4, f32[256]{0:T(256)S(1)} %bitcast.6), kind=kLoop, calls=%fused_computation | loop fusion | flops 3145728 | bytes 3149824 | tf_op jit(solution)/shard_map/convert_element_type | solution.py:528

commit v5 on v4

--- a/solution.py
+++ b/solution.py
@@ -16,8 +16,8 @@
 CORNERS = (0, 1, 2, 3)
 TAPS = range(3)
 EARLY_A = 4
-EARLY_B = 4
-GROUP = 4
+EARLY_B = 2
+GROUP = 2
 
 
 def net_kernel(dims, x, w_a, bn_a, w_down, bn_down, w_b, bn_b, zo, mean_o, inv_o, gain_o, shift_o,

time: 72.2 us -> 69.2 us (0.958)
  Pallas kernels: 70.7 us -> 67.7 us
    pallas_call x1, Pallas kernels: 70.7 us -> 67.7 us  [net(): pl.pallas_call(functools.partial(net_kernel, (rows_n, cols_n, n_img, heig...]
where the time goes in v5:
time: 69.2 us; the launch traced here: 69.1 us
  Pallas kernels  67.7 us (98%)
  other arithmetic  1.37 us (2%)
    pallas_call x1, Pallas kernels, net(): pl.pallas_call(functools.partial(net_kernel, (rows_n, cols_n, n_img, heig...  67.7 us

profile of v5, /device:TPU:97, one launch (start us, length us, event | category | flops | bytes accessed | tf_op | source)
XLA Modules:
  0.0 69.1 jit_solution(17851584081525211746)
XLA Ops:
  0.0 67.7 %conv_bn_net.1 = (f32[8,4,64,256]{3,2,1,0:T(8,128)S(1)}, f32[1,256]{1,0:T(1,128)S(1)}, f32[1,256]{1,0:T(1,128)S(1)}, f32[1,256]{1,0:T(1,128)S(1)}, f32[1,256]{1,0:T(1,128)S(1)}) custom-call(bf16[8,8,128,128]{3,2,1,0:T(8,128)(2,1)} %x.1, bf16[3,3,3,128,128]{4,3,2,1,0:T(8,128)(2,1)} %w_a.1, f32[3,2,128]{2,1,0:T(2,128)} %bn_a.1, ...), custom_call_target="tpu_custom_call" | custom-call | tf_op jit(solution)/shard_map/conv_bn_net/pallas_call | solution.py:518
  67.8 1.4 %maximum_convert_fusion = bf16[8,4,64,256]{3,2,1,0:T(8,128)(2,1)} fusion(f32[8,4,64,256]{3,2,1,0:T(8,128)S(1)} %get-tuple-element.11, f32[256]{0:T(256)S(1)} %bitcast.7, f32[256]{0:T(256)S(1)} %bitcast.5, f32[256]{0:T(256)S(1)} %bitcast.4, f32[256]{0:T(256)S(1)} %bitcast.6), kind=kLoop, calls=%fused_computation | loop fusion | flops 3145728 | bytes 3149824 | tf_op jit(solution)/shard_map/convert_element_type | solution.py:528

commit v6 on v5

--- a/solution.py
+++ b/solution.py
@@ -17,7 +17,6 @@
 TAPS = range(3)
 EARLY_A = 4
 EARLY_B = 2
-GROUP = 2
 
 
 def net_kernel(dims, x, w_a, bn_a, w_down, bn_down, w_b, bn_b, zo, mean_o, inv_o, gain_o, shift_o,
@@ -67,15 +66,21 @@
     while 2 * steps[-1] < max(rows_n, cols_n) and len(steps) < meet.shape[0]:
         steps.append(2 * steps[-1])
 
+    def meet_again(k):
+        if k < len(steps):
+            hear(meet.at[k], steps[k])
+        if k + 1 < len(steps):
+            call(meet.at[k + 1], steps[k + 1])
+
     barrier = pltpu.get_barrier_semaphore()
     call(barrier, 1)
 
     chips = rows_n // 2
     chip, core = lax.div(sp, 2), lax.rem(sp, 2)
-    lines = [[lax.rem(chip + d, chips) * 2 + c for c in (core, 1 - core)] for d in range(chips)]
-    files = [lax.rem(sp2 + d, cols_n) for d in range(cols_n)]
-    hops = {(dx, dy): min(dx, chips - dx) + min(dy, cols_n - dy) for dx in range(chips) for dy in range(cols_n)}
-    others = [{"sp": lines[dx][flip], "sp2": files[dy]} for dx, dy in sorted(hops, key=lambda o: -hops[o]) for flip in (1, 0) if (dx, dy, flip) != (0, 0, 0)]
+    others = []
+    for d in sorted(range(chips), key=lambda d: -min(d, chips - d)):
+        at = lax.rem(chip + d, chips) * 2
+        others.append((at + 1 - core, at + core))
 
     for i in range(n_img):
         pltpu.make_async_copy(x.at[i], xin.at[i], in_sem.at[i]).start()
@@ -205,8 +210,19 @@
         buf = sums_refs(e)
         buf[me] = part
 
-        for other in others:
-            pltpu.make_async_remote_copy(buf.at[me], buf.at[me], st_send.at[e], st_recv.at[e], device_id=other, device_id_type=MESH).start()
+        def send(to_sp, to_sp2):
+            pltpu.make_async_remote_copy(buf.at[me], buf.at[me], st_send.at[e], st_recv.at[e], device_id={"sp": to_sp, "sp2": to_sp2},
+                                         device_id_type=MESH).start()
+
+        for k, pair in enumerate(others):
+            def send_file(t, carry, pair=pair):
+                to_sp2 = lax.rem(sp2 + cols_n // 2 + lax.select(lax.rem(t, 2) == 0, lax.div(t + 1, 2), -lax.div(t + 1, 2)), cols_n)
+                for to_sp in pair:
+                    send(to_sp, to_sp2)
+                return carry
+
+            lax.fori_loop(0, cols_n if k + 1 < len(others) else cols_n - 1, send_file, 0)
+        send(others[-1][0], sp2)
 
     def finish_sums(e, num_pos):
         buf = sums_refs(e)
@@ -380,23 +396,34 @@
         wait_rows(e, in_sides, (0,))
         prep(0, 0)
 
-        def group(j, carry):
-            i = GROUP * j
-            wait_rows(e, in_sides, [i + u for u in range(1, GROUP)])
-            wait_rows(e, in_sides, (i + GROUP,), i + GROUP < n_img)
-            for u in range(GROUP):
-                nxt = u + 1
-                prep(i + nxt if nxt < GROUP else lax.min(i + nxt, n_img - 1), nxt % 2)
-                carry = conv(i + u, u % 2, carry)
-            send_rows(e + 1, out_sides, [i + u for u in range(GROUP)], i < early)
+        half = n_img // 2
+
+        def pair(j, carry):
+            i = 2 * j
+            wait_rows(e, in_sides, (i + 1, i + 2))
+            for u in SIDES:
+                prep(i + u + 1, 1 - u)
+                carry = conv(i + u, u, carry)
+            send_rows(e + 1, out_sides, (i, i + 1), i < early)
             return carry
 
-        s1, s2 = lax.fori_loop(0, n_img // GROUP, group, zero_sums)
+        carry = lax.fori_loop(0, half // 2, pair, zero_sums)
+        wait_rows(e, in_sides, range(half + 1, n_img))
+        if e == 0:
+            meet_again(1)
+        for i in range(half, n_img):
+            if i + 1 < n_img:
+                prep(i + 1, (i + 1) % 2)
+            carry = conv(i, i % 2, carry)
+        s1, s2 = carry
         s1, s2 = (jnp.sum(s, axis=0, keepdims=True) for s in (s1, s2))
         if e < 3:
             part = [s1[:, 0:chan] + s1[:, chan:], s2[:, 0:chan] + s2[:, chan:]]
         else:
             part = [s1[:, 0:chan], s1[:, chan:], s2[:, 0:chan], s2[:, chan:]]
+        if e == 0:
+            for k in range(2, len(steps)):
+                meet_again(k)
         start_sums(e, jnp.concatenate(part, axis=0))
         if e < 5:
             both = len(out_sides) == 2
@@ -408,10 +435,7 @@
     send_rows(0, SIDES, range(n_img))
     for copy in weight_copies[:6]:
         copy.wait()
-    for k, step in enumerate(steps):
-        hear(meet.at[k], step)
-        if k + 1 < len(steps):
-            call(meet.at[k + 1], steps[k + 1])
+    meet_again(0)
     wait_cols(0)
 
     pos_a = n_dev * n_img * height * width

time: 69.2 us -> 66.8 us (0.965)
  Pallas kernels: 67.7 us -> 65.4 us
    pallas_call x1, Pallas kernels: 67.7 us -> 65.4 us  [net(): pl.pallas_call(functools.partial(net_kernel, (rows_n, cols_n, n_img, heig...]
where the time goes in v6:
time: 66.8 us
  Pallas kernels  65.4 us (98%)
  other arithmetic  1.37 us (2%)
    pallas_call x1, Pallas kernels, net(): pl.pallas_call(functools.partial(net_kernel, (rows_n, cols_n, n_img, heig...  65.4 us
    convert_element_type x1, other arithmetic, net(): return jnp.maximum(gain * (z - mean) * inv + shift, 0.0).astype(BF16)  1.37 us

profile of v6, /device:TPU:97, one launch (start us, length us, event | category | flops | bytes accessed | tf_op | source)
XLA Modules:
  0.0 66.8 jit_solution(10980768134324981210)
XLA Ops:
  0.0 65.4 %conv_bn_net.1 = (f32[8,4,64,256]{3,2,1,0:T(8,128)S(1)}, f32[1,256]{1,0:T(1,128)S(1)}, f32[1,256]{1,0:T(1,128)S(1)}, f32[1,256]{1,0:T(1,128)S(1)}, f32[1,256]{1,0:T(1,128)S(1)}) custom-call(bf16[8,8,128,128]{3,2,1,0:T(8,128)(2,1)} %x.1, bf16[3,3,3,128,128]{4,3,2,1,0:T(8,128)(2,1)} %w_a.1, f32[3,2,128]{2,1,0:T(2,128)} %bn_a.1, ...), custom_call_target="tpu_custom_call" | custom-call | tf_op jit(solution)/shard_map/conv_bn_net/pallas_call | solution.py:542
  65.4 1.4 %maximum_convert_fusion = bf16[8,4,64,256]{3,2,1,0:T(8,128)(2,1)} fusion(f32[8,4,64,256]{3,2,1,0:T(8,128)S(1)} %get-tuple-element.11, f32[256]{0:T(256)S(1)} %bitcast.7, f32[256]{0:T(256)S(1)} %bitcast.5, f32[256]{0:T(256)S(1)} %bitcast.4, f32[256]{0:T(256)S(1)} %bitcast.6), kind=kLoop, calls=%fused_computation | loop fusion | flops 3145728 | bytes 3149824 | tf_op jit(solution)/shard_map/convert_element_type | solution.py:552

commit v7 on v6

--- a/solution.py
+++ b/solution.py
@@ -15,7 +15,7 @@
 SIDES = (0, 1)
 CORNERS = (0, 1, 2, 3)
 TAPS = range(3)
-EARLY_A = 4
+EARLY_A = 2
 EARLY_B = 2
 
 
@@ -72,9 +72,6 @@
         if k + 1 < len(steps):
             call(meet.at[k + 1], steps[k + 1])
 
-    barrier = pltpu.get_barrier_semaphore()
-    call(barrier, 1)
-
     chips = rows_n // 2
     chip, core = lax.div(sp, 2), lax.rem(sp, 2)
     others = []
@@ -98,13 +95,8 @@
     for copy in weight_copies:
         copy.start()
 
-    zeros = jnp.zeros((chan, chan), BF16)
-    for layer in TAPS:
-        for ky in TAPS:
-            ws[layer, ky, 0:chan, chan:wide] = zeros
-            ws[layer, ky, chan:wide, 0:chan] = zeros
-    for ky in TAPS:
-        wd[ky, 1, 0:chan, :] = jnp.zeros((chan, wide), BF16)
+    barrier = pltpu.get_barrier_semaphore()
+    call(barrier, 1)
 
     for i in range(n_img):
         pltpu.make_async_copy(x.at[i], xin.at[i], in_sem.at[i]).wait()
@@ -228,7 +220,7 @@
         buf = sums_refs(e)
         rest = buf.at[pl.ds(0, n_dev - 1)]
         pltpu.make_async_copy(rest, rest, st_recv.at[e]).wait()
-        total = jnp.sum(buf[...], axis=0) / num_pos
+        total = jnp.sum(buf[...], axis=0) * (1.0 / num_pos)
         lines = total.shape[0] // 2
         mean = total[0:lines]
         var = total[lines:] - mean * mean
@@ -398,24 +390,22 @@
 
         half = n_img // 2
 
-        def pair(j, carry):
-            i = 2 * j
-            wait_rows(e, in_sides, (i + 1, i + 2))
-            for u in SIDES:
-                prep(i + u + 1, 1 - u)
-                carry = conv(i + u, u, carry)
-            send_rows(e + 1, out_sides, (i, i + 1), i < early)
+        def group(j, carry):
+            i = half * j
+            wait_rows(e, in_sides, [i + u for u in range(1, half)])
+            wait_rows(e, in_sides, (i + half,), j == 0)
+            if e == 0:
+                @pl.when(j == 1)
+                def _():
+                    meet_again(1)
+            for u in range(half):
+                nxt = u + 1
+                prep(i + nxt if nxt < half else half, nxt % 2)
+                carry = conv(i + u, u % 2, carry)
+            send_rows(e + 1, out_sides, range(early), j == 0)
             return carry
 
-        carry = lax.fori_loop(0, half // 2, pair, zero_sums)
-        wait_rows(e, in_sides, range(half + 1, n_img))
-        if e == 0:
-            meet_again(1)
-        for i in range(half, n_img):
-            if i + 1 < n_img:
-                prep(i + 1, (i + 1) % 2)
-            carry = conv(i, i % 2, carry)
-        s1, s2 = carry
+        s1, s2 = lax.fori_loop(0, 2, group, zero_sums)
         s1, s2 = (jnp.sum(s, axis=0, keepdims=True) for s in (s1, s2))
         if e < 3:
             part = [s1[:, 0:chan] + s1[:, chan:], s2[:, 0:chan] + s2[:, chan:]]
@@ -430,9 +420,16 @@
             start_cols(e + 1, SIDES if both else (0,), CORNERS if both else (0,))
             send_rows(e + 1, out_sides, range(early, n_img))
 
-    call(meet.at[0], steps[0])
     start_cols(0)
     send_rows(0, SIDES, range(n_img))
+    call(meet.at[0], steps[0])
+    zeros = jnp.zeros((chan, chan), BF16)
+    for depth in TAPS:
+        for ky in TAPS:
+            ws[depth, ky, 0:chan, chan:wide] = zeros
+            ws[depth, ky, chan:wide, 0:chan] = zeros
+    for ky in TAPS:
+        wd[ky, 1, 0:chan, :] = jnp.zeros((chan, wide), BF16)
     for copy in weight_copies[:6]:
         copy.wait()
     meet_again(0)

time: 66.8 us -> 68.6 us (1.027)
  Pallas kernels: 65.4 us -> 67.1 us
    pallas_call x1, Pallas kernels: 65.4 us -> 67.1 us  [net(): pl.pallas_call(functools.partial(net_kernel, (rows_n, cols_n, n_img, heig...]
where the time goes in v7:
time: 68.6 us; the launch traced here: 68.5 us
  Pallas kernels  67.1 us (98%)
  other arithmetic  1.37 us (2%)
    pallas_call x1, Pallas kernels, net(): pl.pallas_call(functools.partial(net_kernel, (rows_n, cols_n, n_img, heig...  67.1 us
    convert_element_type x1, other arithmetic, net(): return jnp.maximum(gain * (z - mean) * inv + shift, 0.0).astype(BF16)  1.37 us

profile of v7, /device:TPU:97, one launch (start us, length us, event | category | flops | bytes accessed | tf_op | source)
XLA Modules:
  0.0 68.5 jit_solution(12622871314777693026)
XLA Ops:
  0.0 67.1 %conv_bn_net.1 = (f32[8,4,64,256]{3,2,1,0:T(8,128)S(1)}, f32[1,256]{1,0:T(1,128)S(1)}, f32[1,256]{1,0:T(1,128)S(1)}, f32[1,256]{1,0:T(1,128)S(1)}, f32[1,256]{1,0:T(1,128)S(1)}) custom-call(bf16[8,8,128,128]{3,2,1,0:T(8,128)(2,1)} %x.1, bf16[3,3,3,128,128]{4,3,2,1,0:T(8,128)(2,1)} %w_a.1, f32[3,2,128]{2,1,0:T(2,128)} %bn_a.1, ...), custom_call_target="tpu_custom_call" | custom-call | tf_op jit(solution)/shard_map/conv_bn_net/pallas_call | solution.py:539
  67.1 1.4 %maximum_convert_fusion = bf16[8,4,64,256]{3,2,1,0:T(8,128)(2,1)} fusion(f32[8,4,64,256]{3,2,1,0:T(8,128)S(1)} %get-tuple-element.11, f32[256]{0:T(256)S(1)} %bitcast.7, f32[256]{0:T(256)S(1)} %bitcast.5, f32[256]{0:T(256)S(1)} %bitcast.4, f32[256]{0:T(256)S(1)} %bitcast.6), kind=kLoop, calls=%fused_computation | loop fusion | flops 3145728 | bytes 3149824 | tf_op jit(solution)/shard_map/convert_element_type | solution.py:549

commit v8 on v6

--- a/solution.py
+++ b/solution.py
@@ -16,7 +16,7 @@
 CORNERS = (0, 1, 2, 3)
 TAPS = range(3)
 EARLY_A = 4
-EARLY_B = 2
+EARLY_B = 4
 
 
 def net_kernel(dims, x, w_a, bn_a, w_down, bn_down, w_b, bn_b, zo, mean_o, inv_o, gain_o, shift_o,
@@ -72,9 +72,6 @@
         if k + 1 < len(steps):
             call(meet.at[k + 1], steps[k + 1])
 
-    barrier = pltpu.get_barrier_semaphore()
-    call(barrier, 1)
-
     chips = rows_n // 2
     chip, core = lax.div(sp, 2), lax.rem(sp, 2)
     others = []
@@ -98,13 +95,8 @@
     for copy in weight_copies:
         copy.start()
 
-    zeros = jnp.zeros((chan, chan), BF16)
-    for layer in TAPS:
-        for ky in TAPS:
-            ws[layer, ky, 0:chan, chan:wide] = zeros
-            ws[layer, ky, chan:wide, 0:chan] = zeros
-    for ky in TAPS:
-        wd[ky, 1, 0:chan, :] = jnp.zeros((chan, wide), BF16)
+    barrier = pltpu.get_barrier_semaphore()
+    call(barrier, 1)
 
     for i in range(n_img):
         pltpu.make_async_copy(x.at[i], xin.at[i], in_sem.at[i]).wait()
@@ -228,7 +220,7 @@
         buf = sums_refs(e)
         rest = buf.at[pl.ds(0, n_dev - 1)]
         pltpu.make_async_copy(rest, rest, st_recv.at[e]).wait()
-        total = jnp.sum(buf[...], axis=0) / num_pos
+        total = jnp.sum(buf[...], axis=0) * (1.0 / num_pos)
         lines = total.shape[0] // 2
         mean = total[0:lines]
         var = total[lines:] - mean * mean
@@ -430,9 +422,16 @@
             start_cols(e + 1, SIDES if both else (0,), CORNERS if both else (0,))
             send_rows(e + 1, out_sides, range(early, n_img))
 
-    call(meet.at[0], steps[0])
     start_cols(0)
     send_rows(0, SIDES, range(n_img))
+    call(meet.at[0], steps[0])
+    zeros = jnp.zeros((chan, chan), BF16)
+    for depth in TAPS:
+        for ky in TAPS:
+            ws[depth, ky, 0:chan, chan:wide] = zeros
+            ws[depth, ky, chan:wide, 0:chan] = zeros
+    for ky in TAPS:
+        wd[ky, 1, 0:chan, :] = jnp.zeros((chan, wide), BF16)
     for copy in weight_copies[:6]:
         copy.wait()
     meet_again(0)

time: 66.8 us -> 66.8 us (level)
  no operation moved by 1% of the time
where the time goes in v8:
time: 66.8 us; the launch traced here: 66.7 us
  Pallas kernels  65.4 us (98%)
  other arithmetic  1.37 us (2%)
    pallas_call x1, Pallas kernels, net(): pl.pallas_call(functools.partial(net_kernel, (rows_n, cols_n, n_img, heig...  65.4 us
    convert_element_type x1, other arithmetic, net(): return jnp.maximum(gain * (z - mean) * inv + shift, 0.0).astype(BF16)  1.37 us

profile of v8, /device:TPU:97, one launch (start us, length us, event | category | flops | bytes accessed | tf_op | source)
XLA Modules:
  0.0 66.7 jit_solution(17511711820131570523)
XLA Ops:
  0.0 65.4 %conv_bn_net.1 = (f32[8,4,64,256]{3,2,1,0:T(8,128)S(1)}, f32[1,256]{1,0:T(1,128)S(1)}, f32[1,256]{1,0:T(1,128)S(1)}, f32[1,256]{1,0:T(1,128)S(1)}, f32[1,256]{1,0:T(1,128)S(1)}) custom-call(bf16[8,8,128,128]{3,2,1,0:T(8,128)(2,1)} %x.1, bf16[3,3,3,128,128]{4,3,2,1,0:T(8,128)(2,1)} %w_a.1, f32[3,2,128]{2,1,0:T(2,128)} %bn_a.1, ...), custom_call_target="tpu_custom_call" | custom-call | tf_op jit(solution)/shard_map/conv_bn_net/pallas_call | solution.py:541
  65.4 1.4 %maximum_convert_fusion = bf16[8,4,64,256]{3,2,1,0:T(8,128)(2,1)} fusion(f32[8,4,64,256]{3,2,1,0:T(8,128)S(1)} %get-tuple-element.11, f32[256]{0:T(256)S(1)} %bitcast.7, f32[256]{0:T(256)S(1)} %bitcast.5, f32[256]{0:T(256)S(1)} %bitcast.4, f32[256]{0:T(256)S(1)} %bitcast.6), kind=kLoop, calls=%fused_computation | loop fusion | flops 3145728 | bytes 3149824 | tf_op jit(solution)/shard_map/convert_element_type | solution.py:551

commit v9 on v8

--- a/solution.py
+++ b/solution.py
@@ -15,8 +15,8 @@
 SIDES = (0, 1)
 CORNERS = (0, 1, 2, 3)
 TAPS = range(3)
-EARLY_A = 4
-EARLY_B = 4
+EARLY_A = 2
+EARLY_B = 2
 
 
 def net_kernel(dims, x, w_a, bn_a, w_down, bn_down, w_b, bn_b, zo, mean_o, inv_o, gain_o, shift_o,

time: 66.8 us -> 68.3 us (1.022)
  Pallas kernels: 65.4 us -> 66.8 us
    pallas_call x1, Pallas kernels: 65.4 us -> 66.8 us  [net(): pl.pallas_call(functools.partial(net_kernel, (rows_n, cols_n, n_img, heig...]
where the time goes in v9:
time: 68.3 us; the launch traced here: 68.2 us
  Pallas kernels  66.8 us (98%)
  other arithmetic  1.37 us (2%)
    pallas_call x1, Pallas kernels, net(): pl.pallas_call(functools.partial(net_kernel, (rows_n, cols_n, n_img, heig...  66.8 us
    convert_element_type x1, other arithmetic, net(): return jnp.maximum(gain * (z - mean) * inv + shift, 0.0).astype(BF16)  1.37 us

profile of v9, /device:TPU:97, one launch (start us, length us, event | category | flops | bytes accessed | tf_op | source)
XLA Modules:
  0.0 68.2 jit_solution(1090204269103807230)
XLA Ops:
  0.0 66.8 %conv_bn_net.1 = (f32[8,4,64,256]{3,2,1,0:T(8,128)S(1)}, f32[1,256]{1,0:T(1,128)S(1)}, f32[1,256]{1,0:T(1,128)S(1)}, f32[1,256]{1,0:T(1,128)S(1)}, f32[1,256]{1,0:T(1,128)S(1)}) custom-call(bf16[8,8,128,128]{3,2,1,0:T(8,128)(2,1)} %x.1, bf16[3,3,3,128,128]{4,3,2,1,0:T(8,128)(2,1)} %w_a.1, f32[3,2,128]{2,1,0:T(2,128)} %bn_a.1, ...), custom_call_target="tpu_custom_call" | custom-call | tf_op jit(solution)/shard_map/conv_bn_net/pallas_call | solution.py:541
  66.9 1.4 %maximum_convert_fusion = bf16[8,4,64,256]{3,2,1,0:T(8,128)(2,1)} fusion(f32[8,4,64,256]{3,2,1,0:T(8,128)S(1)} %get-tuple-element.11, f32[256]{0:T(256)S(1)} %bitcast.7, f32[256]{0:T(256)S(1)} %bitcast.5, f32[256]{0:T(256)S(1)} %bitcast.4, f32[256]{0:T(256)S(1)} %bitcast.6), kind=kLoop, calls=%fused_computation | loop fusion | flops 3145728 | bytes 3149824 | tf_op jit(solution)/shard_map/convert_element_type | solution.py:551

commit v10 on v9

--- a/solution.py
+++ b/solution.py
@@ -15,8 +15,8 @@
 SIDES = (0, 1)
 CORNERS = (0, 1, 2, 3)
 TAPS = range(3)
-EARLY_A = 2
-EARLY_B = 2
+EARLY_A = 3
+EARLY_B = 3
 
 
 def net_kernel(dims, x, w_a, bn_a, w_down, bn_down, w_b, bn_b, zo, mean_o, inv_o, gain_o, shift_o,
@@ -396,7 +396,8 @@
             for u in SIDES:
                 prep(i + u + 1, 1 - u)
                 carry = conv(i + u, u, carry)
-            send_rows(e + 1, out_sides, (i, i + 1), i < early)
+            for u in SIDES:
+                send_rows(e + 1, out_sides, (i + u,), i + u < early)
             return carry
 
         carry = lax.fori_loop(0, half // 2, pair, zero_sums)

time: 68.3 us -> 66 us (0.966)
  Pallas kernels: 66.8 us -> 64.5 us
    pallas_call x1, Pallas kernels: 66.8 us -> 64.5 us  [net(): pl.pallas_call(functools.partial(net_kernel, (rows_n, cols_n, n_img, heig...]
where the time goes in v10:
time: 66 us; the launch traced here: 65.9 us
  Pallas kernels  64.5 us (98%)
  other arithmetic  1.37 us (2%)
    pallas_call x1, Pallas kernels, net(): pl.pallas_call(functools.partial(net_kernel, (rows_n, cols_n, n_img, heig...  64.5 us
    convert_element_type x1, other arithmetic, net(): return jnp.maximum(gain * (z - mean) * inv + shift, 0.0).astype(BF16)  1.37 us

profile of v10, /device:TPU:97, one launch (start us, length us, event | category | flops | bytes accessed | tf_op | source)
XLA Modules:
  0.0 65.9 jit_solution(15388382693251341515)
XLA Ops:
  0.0 64.5 %conv_bn_net.1 = (f32[8,4,64,256]{3,2,1,0:T(8,128)S(1)}, f32[1,256]{1,0:T(1,128)S(1)}, f32[1,256]{1,0:T(1,128)S(1)}, f32[1,256]{1,0:T(1,128)S(1)}, f32[1,256]{1,0:T(1,128)S(1)}) custom-call(bf16[8,8,128,128]{3,2,1,0:T(8,128)(2,1)} %x.1, bf16[3,3,3,128,128]{4,3,2,1,0:T(8,128)(2,1)} %w_a.1, f32[3,2,128]{2,1,0:T(2,128)} %bn_a.1, ...), custom_call_target="tpu_custom_call" | custom-call | tf_op jit(solution)/shard_map/conv_bn_net/pallas_call | solution.py:542
  64.5 1.4 %maximum_convert_fusion = bf16[8,4,64,256]{3,2,1,0:T(8,128)(2,1)} fusion(f32[8,4,64,256]{3,2,1,0:T(8,128)S(1)} %get-tuple-element.11, f32[256]{0:T(256)S(1)} %bitcast.7, f32[256]{0:T(256)S(1)} %bitcast.5, f32[256]{0:T(256)S(1)} %bitcast.4, f32[256]{0:T(256)S(1)} %bitcast.6), kind=kLoop, calls=%fused_computation | loop fusion | flops 3145728 | bytes 3149824 | tf_op jit(solution)/shard_map/convert_element_type | solution.py:552

commit v11 on v10

--- a/solution.py
+++ b/solution.py
@@ -385,7 +385,6 @@
         return add_sums(acc, carry)
 
     def layer(e, prep, conv, in_sides, out_sides, early):
-        wait_rows(e, in_sides, (0,))
         prep(0, 0)
 
         half = n_img // 2
@@ -452,6 +451,7 @@
         return mean, inv, gain, shift
 
     part = functools.partial
+    wait_rows(0, SIDES, SIDES[:1])
     layer(0, prep_x, part(conv_a, 0), SIDES, SIDES, EARLY_A)
 
     for copy in weight_copies[6:]:
@@ -459,26 +459,31 @@
     wait_row_sends(0)
     wait_col_sends(0)
     wait_cols(1)
+    wait_rows(1, SIDES, SIDES[:1])
     layer(1, part(norm_a, 1, params_a(0, 0)), part(conv_a, 1), SIDES, SIDES, EARLY_A)
 
     wait_row_sends(1)
     wait_col_sends(1)
     wait_cols(2)
+    wait_rows(2, SIDES, SIDES[:1])
     layer(2, part(norm_a, 2, params_a(1, 1)), part(conv_a, 2), SIDES, (0,), EARLY_A)
 
     wait_row_sends(2)
     wait_col_sends(2)
     wait_cols(3, (1,), (3,))
+    wait_rows(3, SIDES[1:], SIDES[:1])
     layer(3, part(norm_a, 3, params_a(2, 2), up=False), conv_down, (1,), SIDES, EARLY_B)
 
     wait_row_sends(3, (0,))
     wait_col_sends(3, (0,), (0,))
     wait_cols(4)
+    wait_rows(4, SIDES, SIDES[:1])
     layer(4, part(norm_b, 4, params_b(3, gd)), part(conv_b, 0), SIDES, SIDES, EARLY_B)
 
     wait_row_sends(4)
     wait_col_sends(4)
     wait_cols(5)
+    wait_rows(5, SIDES, SIDES[:1])
     layer(5, part(norm_b, 5, params_b(4, gb.at[0])), part(conv_b, 1), SIDES, (), 0)
 
     wait_row_sends(5)

time: 66 us -> 66 us (level)
  no operation moved by 1% of the time
where the time goes in v11:
time: 66 us; the launch traced here: 65.9 us
  Pallas kernels  64.5 us (98%)
  other arithmetic  1.37 us (2%)
    pallas_call x1, Pallas kernels, net(): pl.pallas_call(functools.partial(net_kernel, (rows_n, cols_n, n_img, heig...  64.5 us
    convert_element_type x1, other arithmetic, net(): return jnp.maximum(gain * (z - mean) * inv + shift, 0.0).astype(BF16)  1.37 us

profile of v11, /device:TPU:97, one launch (start us, length us, event | category | flops | bytes accessed | tf_op | source)
XLA Modules:
  0.0 65.9 jit_solution(2644261280427482187)
XLA Ops:
  0.0 64.5 %conv_bn_net.1 = (f32[8,4,64,256]{3,2,1,0:T(8,128)S(1)}, f32[1,256]{1,0:T(1,128)S(1)}, f32[1,256]{1,0:T(1,128)S(1)}, f32[1,256]{1,0:T(1,128)S(1)}, f32[1,256]{1,0:T(1,128)S(1)}) custom-call(bf16[8,8,128,128]{3,2,1,0:T(8,128)(2,1)} %x.1, bf16[3,3,3,128,128]{4,3,2,1,0:T(8,128)(2,1)} %w_a.1, f32[3,2,128]{2,1,0:T(2,128)} %bn_a.1, ...), custom_call_target="tpu_custom_call" | custom-call | tf_op jit(solution)/shard_map/conv_bn_net/pallas_call | solution.py:547
  64.5 1.4 %maximum_convert_fusion = bf16[8,4,64,256]{3,2,1,0:T(8,128)(2,1)} fusion(f32[8,4,64,256]{3,2,1,0:T(8,128)S(1)} %get-tuple-element.11, f32[256]{0:T(256)S(1)} %bitcast.7, f32[256]{0:T(256)S(1)} %bitcast.5, f32[256]{0:T(256)S(1)} %bitcast.4, f32[256]{0:T(256)S(1)} %bitcast.6), kind=kLoop, calls=%fused_computation | loop fusion | flops 3145728 | bytes 3149824 | tf_op jit(solution)/shard_map/convert_element_type | solution.py:557
